TPU v7x, 256 devices: a whole 4x4x8 slice. The times are simulated.
256 devices in a mesh: ka: 32 (over z_hi, x, y), ga: 8 (over z_lo, core).
Axes of the slice: x: 4, y: 4, z: 8 (z_hi: 2, z_lo: 4; z = z_hi * 4 + z_lo), core: 2. Of those that a mesh axis runs over, the one named last changes fastest.
Arguments:
- psi: bfloat16 [32, 2, 128, 2048], P('ka', None, None, 'ga'), may hold values from -0.62890625 to 0.62890625
- dvscf: bfloat16 [96, 2, 2048], P(None, None, 'ga'), may hold values from -6 to 6
- kq_map: int32 [32], P('ka'), may hold values from 0 to 31, each once
Outputs:
- coupling: float32 [96, 32, 2, 128, 128], P('ga', 'ka')
Inputs may be any that keep to these rules, and one draw needn't show every extreme that they name: kq_map is a permutation of the k-points 0 to 31.
All inputs are finite; a program needn't handle non-finite values.
Results may differ from a plain program's by a relative error of at most 0.0029.
Values may be sent and summed in bfloat16 or wider, within the bound.
No kernel may reach another device: no remote copies, remote signals or barrier semaphores. Data moves between devices by JAX's collectives and lax.ppermute only.
A program may use at most 128 MiB of HBM per device.

v0:
```python
import jax
import jax.numpy as jnp
from jax import lax
from jax.experimental import pallas as pl
from jax.experimental.pallas import tpu as pltpu
from jax.sharding import Mesh
from jax.sharding import PartitionSpec as P

KA = ("zh", "x", "y")
GA = ("zl", "c")
XY = ("x", "y")
SWAP = [(0, 1), (1, 0)]
MIRROR = [(z, 7 - z) for z in range(8)]
STEPS = (0, 1, 3, 2)
TAG = 8
SMALL = pltpu.CompilerParams(vmem_limit_bytes=20 * 2**20)
IN_SMEM = pl.BlockSpec(memory_space=pltpu.SMEM)
IN_VMEM = pl.BlockSpec(memory_space=pltpu.VMEM)


def ring(step, size=4):
    return [(i, (i + step) % size) for i in range(size)]


def pack_lines(slab, potential):
    rows, cells = slab.shape
    modes = potential.shape[0] // 4

    def kernel(slab_ref, pot_ref, *outs):
        zl = lax.axis_index("zl")
        for s, out in zip(STEPS, outs):
            out[:rows] = slab_ref[...]
            first = modes * lax.rem(zl + s, 4)
            for m in range(modes):
                out[rows + 2 * m : rows + 2 * m + 2] = pot_ref[first + m]

    return pl.pallas_call(
        kernel,
        in_specs=[IN_VMEM, IN_VMEM],
        out_shape=[jax.ShapeDtypeStruct((rows + 2 * modes, cells), slab.dtype)] * 4,
        compiler_params=SMALL,
    )(slab, potential)


def pack_spread(slab, kq):
    rows, cells = slab.shape
    piece = rows // 16

    def kernel(kq_ref, slab_ref, out):
        tag = jnp.full((TAG, cells), kq_ref[0].astype(jnp.float32)).astype(slab.dtype)
        for j in range(16):
            out[j, :piece] = slab_ref[j * piece : (j + 1) * piece]
            out[j, piece:] = tag

    return pl.pallas_call(
        kernel,
        in_specs=[IN_SMEM, IN_VMEM],
        out_shape=jax.ShapeDtypeStruct((16, piece + TAG, cells), slab.dtype),
        compiler_params=SMALL,
    )(kq, slab)


def strip(tagged):
    count, rows, cells = tagged.shape

    def kernel(ref, out):
        out[...] = ref[:, : rows - TAG]

    return pl.pallas_call(
        kernel,
        in_specs=[IN_VMEM],
        out_shape=jax.ShapeDtypeStruct((count, rows - TAG, cells), tagged.dtype),
        compiler_params=SMALL,
    )(tagged)


def choose(tagged, swapped):
    count, piece, _ = swapped.shape

    def kernel(ref, swapped_ref, out):
        zh = lax.axis_index("zh")
        for d in range(count):
            source = jnp.max(ref[d, piece:, :128].astype(jnp.float32)).astype(jnp.int32)
            block = lax.rem(source, count)
            out[d] = jnp.where(source // count == zh, ref[block, :piece], swapped_ref[block])

    return pl.pallas_call(
        kernel,
        in_specs=[IN_VMEM, IN_VMEM],
        out_shape=jax.ShapeDtypeStruct(swapped.shape, swapped.dtype),
        compiler_params=SMALL,
    )(tagged, swapped)


def couple(kq, lines, twins, others, steps, bands, modes, last, before=None):
    parts = len(others)
    half = parts // 2
    cells = others[0].shape[1]
    wide = parts * cells
    rows = 2 * bands
    share = lines.shape[1] - rows
    pairs = modes // 2

    def kernel(kq_ref, lines_ref, twins_ref, *refs):
        other_refs, refs = refs[:parts], refs[parts:]
        if before is not None:
            before_ref, *refs = refs
        out_ref, wave_re, wave_im, pots, left, right_a, right_b, *more = refs
        result, sems = more if last else (out_ref, None)

        def copy(pair):
            at = pl.ds(2 * pair, 2)
            return pltpu.make_async_copy(result.at[at], out_ref.at[at], sems.at[pair])

        first = lax.axis_index("c") * (share // 2)
        zl = lax.axis_index("zl")
        crossed = kq_ref[0] // 16 != lax.axis_index("zh")
        for p in range(parts):
            at = slice(p * cells, (p + 1) * cells)
            s = steps[p % half]
            turned = lax.rem(2 * zl + 5 - s, 4)
            turned = jnp.where(turned == 2, 3, jnp.where(turned == 3, 2, turned))
            index = jnp.where(crossed, turned, STEPS.index(s))
            source = lines_ref if p < half else twins_ref
            wave_re[:, at] = source[index, :bands].astype(jnp.float32)
            wave_im[:, at] = source[index, bands:rows].astype(jnp.float32)
            pots[:, at] = source[index, rows:].astype(jnp.float32)
            left[:, at] = other_refs[p][...]

        def fill(mode, right):
            for p in range(parts):
                at = slice(p * cells, (p + 1) * cells)
                dv_re = pots[pl.ds(first + 2 * mode, 1), at]
                dv_im = pots[pl.ds(first + 2 * mode + 1, 1), at]
                w_re, w_im = wave_re[:, at], wave_im[:, at]
                right[:bands, at] = (dv_re * w_re - dv_im * w_im).astype(jnp.bfloat16)
                right[bands:, at] = (dv_re * w_im + dv_im * w_re).astype(jnp.bfloat16)

        def finish(mode, right):
            full = lax.dot_general(left[...], right[...], (((1,), (1,)), ((), ())), preferred_element_type=jnp.float32)
            real = full[:bands, :bands] + full[bands:, bands:]
            imag = full[:bands, bands:] - full[bands:, :bands]
            if before is not None:
                real, imag = real + before_ref[mode, 0], imag + before_ref[mode, 1]
            result[mode, 0] = real
            result[mode, 1] = imag

        fill(0, right_a)
        for pair in range(pairs):
            fill(2 * pair + 1, right_b)
            finish(2 * pair, right_a)
            if pair + 1 < pairs:
                fill(2 * pair + 2, right_a)
            finish(2 * pair + 1, right_b)
            if last:
                copy(pair).start()
        if last:
            for pair in range(pairs):
                copy(pair).wait()

    total = (modes, 2, bands, bands)
    scratch = [
        pltpu.VMEM((bands, wide), jnp.float32),
        pltpu.VMEM((bands, wide), jnp.float32),
        pltpu.VMEM((share, wide), jnp.float32),
        pltpu.VMEM((rows, wide), jnp.bfloat16),
        pltpu.VMEM((rows, wide), jnp.bfloat16),
        pltpu.VMEM((rows, wide), jnp.bfloat16),
    ]
    if last:
        scratch += [pltpu.VMEM(total, jnp.float32), pltpu.SemaphoreType.DMA((pairs,))]
    args = [kq, lines, twins, *others]
    specs = [IN_SMEM] + [IN_VMEM] * (2 + parts)
    if before is not None:
        args, specs = args + [before], specs + [IN_VMEM]
    return pl.pallas_call(
        kernel,
        in_specs=specs,
        out_specs=pl.BlockSpec(memory_space=pl.ANY) if last else IN_VMEM,
        out_shape=jax.ShapeDtypeStruct(total, jnp.float32),
        scratch_shapes=scratch,
        compiler_params=SMALL,
    )(*args)


def body(psi, dvscf, kq_map):
    bands, cells = psi.shape[2], psi.shape[3]
    modes = dvscf.shape[0] // 8
    slab = psi.reshape(2 * bands, cells)

    tagged = pack_spread(slab, kq_map)
    tagged = lax.all_to_all(tagged, XY, 0, 0, tiled=True)
    packs = pack_lines(slab, dvscf)
    lines = [packs[0]] + [lax.ppermute(packs[i], "zl", ring(STEPS[i])) for i in (1, 2, 3)]
    lines = jnp.stack(lines)
    twins = lax.ppermute(lines, "c", SWAP)
    swapped = lax.ppermute(strip(tagged), ("zh", "zl"), MIRROR)
    phi = lax.all_to_all(choose(tagged, swapped), XY, 0, 0, tiled=True).reshape(2 * bands, cells)

    others = [phi] + [lax.ppermute(phi, "zl", ring(STEPS[i])) for i in (1, 2, 3)]
    mates = [lax.ppermute(o, "c", SWAP) for o in others]
    out = couple(kq_map, lines, twins, others[:1] + mates[:1], STEPS[:1], bands, modes, False)
    out = couple(kq_map, lines, twins, others[1:] + mates[1:], STEPS[1:], bands, modes, True, out)
    return out[:, None]


def solution(mesh):
    finer = Mesh(mesh.devices.reshape(2, 4, 4, 4, 2), KA + GA)
    in_specs = (P(KA, None, None, GA), P(None, None, GA), P(KA))
    out_specs = P(GA, KA, None, None, None)
    return jax.shard_map(body, mesh=finer, in_specs=in_specs, out_specs=out_specs, check_vma=False)
```

profile of v0, /device:TPU:1, one launch (start us, length us, event | category | flops | bytes accessed | tf_op | source)
XLA Modules:
  0.0 63.7 jit_solution(12436551214133056867)
XLA Ops:
  0.0 0.9 %copy-done = bf16[1,2,128,256]{3,2,1,0:T(8,128)(2,1)S(1)} copy-done((bf16[1,2,128,256]{3,2,1,0:T(8,128)(2,1)S(1)}, bf16[1,2,128,256]{3,2,1,0:T(8,128)(2,1)}, u32[]{:S(2)}) %copy-start) | copy-done | bytes 131096
  0.9 0.9 %copy-done.1 = bf16[96,2,256]{2,1,0:T(2,128)(2,1)S(1)} copy-done((bf16[96,2,256]{2,1,0:T(2,128)(2,1)S(1)}, bf16[96,2,256]{2,1,0:T(2,128)(2,1)}, u32[]{:S(2)}) %copy-start.1) | copy-done | bytes 98328
  1.8 0.1 shard_map.37
  1.9 2.5 %collective-permute-start = (bf16[304,256]{1,0:T(8,128)(2,1)S(1)}, bf16[304,256]{1,0:T(8,128)(2,1)S(1)}, u32[]{:S(2)}, u32[]{:S(2)}) collective-permute-start(bf16[304,256]{1,0:T(8,128)(2,1)S(1)} %get-tuple-element.10), channel_id=1, source_target_pairs={{0,2},{2,4},{4,6},{6,0},{1,3},{3,5},{5,7},{7,1},{8,10},{10,12},{12... | collective-permute-start | bytes 466952 | tf_op jit(solution)/shard_map/ppermute | solution.py:194
  4.4 2.8 %collective-permute-start.1 = (bf16[304,256]{1,0:T(8,128)(2,1)S(1)}, bf16[304,256]{1,0:T(8,128)(2,1)S(1)}, u32[]{:S(2)}, u32[]{:S(2)}) collective-permute-start(bf16[304,256]{1,0:T(8,128)(2,1)S(1)} %get-tuple-element.11), channel_id=1, source_target_pairs={{0,6},{2,0},{4,2},{6,4},{1,7},{3,1},{5,3},{7,5},{8,14},{10,8},{12,... | collective-permute-start | bytes 466952 | tf_op jit(solution)/shard_map/ppermute | solution.py:194
  7.2 0.2 collective-permute-start.2
  8.1 0.7 %shard_map.38 = bf16[16,24,256]{2,1,0:T(8,128)(2,1)} custom-call(s32[1]{0:T(128)S(6)} %copy.5.kq_ref, bf16[256,256]{1,0:T(8,128)(2,1)S(1)} %bitcast.10), custom_call_target="tpu_custom_call" | custom-call | tf_op jit(solution)/shard_map/pallas_call | solution.py:55
  8.8 6.8 %all-to-all-start = ((bf16[16,24,256]{2,1,0:T(8,128)(2,1)}), bf16[16,24,256]{2,1,0:T(8,128)(2,1)S(1)}, u32[]{:S(2)}, u32[]{:S(2)}) async-start(bf16[16,24,256]{2,1,0:T(8,128)(2,1)} %shard_map.38), calls=%async_computation | async-start | bytes 393216 | tf_op jit(solution)/shard_map/all_to_all | solution.py:192
  15.5 0.0 collective-permute-done
  15.6 0.0 collective-permute-done.1
  15.6 6.1 %collective-permute-done.2 = bf16[304,256]{1,0:T(8,128)(2,1)S(1)} collective-permute-done((bf16[304,256]{1,0:T(8,128)(2,1)S(1)}, bf16[304,256]{1,0:T(8,128)(2,1)S(1)}, u32[]{:S(2)}, u32[]{:S(2)}) %collective-permute-start.2) | collective-permute-done | bytes 155680 | tf_op jit(solution)/shard_map/ppermute | solution.py:194
  21.6 0.1 pad_maximum_fusion.lines_ref
  21.7 0.6 collective-permute-start.3
  22.3 0.2 all-to-all-done.ref
  22.5 3.8 %collective-permute-start.4 = (bf16[16,16,256]{2,1,0:T(8,128)(2,1)S(1)}, bf16[16,16,256]{2,1,0:T(8,128)(2,1)S(1)}, u32[]{:S(2)}, u32[]{:S(2)}) collective-permute-start(bf16[16,16,256]{2,1,0:T(8,128)(2,1)S(1)} %shard_map.39), channel_id=1, source_target_pairs={{0,134},{2,132},{4,130},{6,128},{128,6},{130,4},{132,2},{134,0},{1... | collective-permute-start | bytes 393224 | tf_op jit(solution)/shard_map/ppermute | solution.py:197
  26.3 2.4 %collective-permute-done.4.swapped_ref = bf16[16,16,256]{2,1,0:T(8,128)(2,1)S(1)} collective-permute-done((bf16[16,16,256]{2,1,0:T(8,128)(2,1)S(1)}, bf16[16,16,256]{2,1,0:T(8,128)(2,1)S(1)}, u32[]{:S(2)}, u32[]{:S(2)}) %collective-permute-start.4) | collective-permute-done | bytes 131104 | tf_op jit(solution)/shard_map/ppermute | solution.py:197
  28.6 0.2 shard_map.40
  28.9 16.9 %all_to_all.10 = bf16[16,16,256]{2,1,0:T(8,128)(2,1)S(1)} all-to-all(bf16[16,16,256]{2,1,0:T(8,128)(2,1)S(1)} %shard_map.40), channel_id=1, replica_groups=mesh['zh'=2,'x'=4,'y'=4,'zl'=4,'c'=2] {'x','y'}, dimensions={0} | all-to-all | bytes 262144 | tf_op jit(solution)/shard_map/all_to_all | solution.py:198
  45.7 0.0 collective-permute-start.7
  45.7 1.1 %collective-permute-start.6 = (bf16[256,256]{1,0:T(8,128)(2,1)S(1)}, bf16[256,256]{1,0:T(8,128)(2,1)S(1)}, u32[]{:S(2)}, u32[]{:S(2)}) collective-permute-start(bf16[256,256]{1,0:T(8,128)(2,1)S(1)} %bitcast.12), channel_id=1, source_target_pairs={{0,6},{2,0},{4,2},{6,4},{1,7},{3,1},{5,3},{7,5},{8,14},{10,8},{12,... | collective-permute-start | bytes 393224 | tf_op jit(solution)/shard_map/ppermute | solution.py:200
  46.8 0.4 collective-permute-start.5
  47.2 2.9 %collective-permute-start.11 = (bf16[256,256]{1,0:T(8,128)(2,1)S(1)}, bf16[256,256]{1,0:T(8,128)(2,1)S(1)}, u32[]{:S(2)}, u32[]{:S(2)}) collective-permute-start(bf16[256,256]{1,0:T(8,128)(2,1)S(1)} %bitcast.14), channel_id=1, source_target_pairs={{0,1},{1,0},{2,3},{3,2},{4,5},{5,4},{6,7},{7,6},{8,9},{9,8},{10,11... | collective-permute-start | bytes 393224 | tf_op jit(solution)/shard_map/ppermute | solution.py:201
  50.1 0.6 collective-permute-done.7.refs_2_
  50.7 7.7 %collective-permute-start.10 = (bf16[256,256]{1,0:T(8,128)(2,1)S(1)}, bf16[256,256]{1,0:T(8,128)(2,1)S(1)}, u32[]{:S(2)}, u32[]{:S(2)}) collective-permute-start(bf16[256,256]{1,0:T(8,128)(2,1)S(1)} %collective-permute-done.7.refs_2_), channel_id=1, source_target_pairs={{0,1},{1,0},{2,3},{3,2},{4,5},{5,4},{6,7},{7,6},{8,9},{9,8},{10,11... | collective-permute-start | bytes 393224 | tf_op jit(solution)/shard_map/ppermute | solution.py:201
  58.3 0.0 collective-permute-done.6.refs_1_
  58.3 0.0 collective-permute-start.9
  58.3 0.0 collective-permute-done.5.refs_0_
  58.3 0.5 collective-permute-start.8
  58.9 1.1 %shard_map.41.refs_6_ = f32[12,2,128,128]{3,2,1,0:T(8,128)S(1)} custom-call(s32[1]{0:T(128)S(6)} %copy.5.kq_ref, bf16[4,304,256]{2,1,0:T(8,128)(2,1)S(1)} %pad_maximum_fusion.lines_ref, bf16[4,304,256]{2,1,0:T(8,128)(2,1)S(1)} %collective-permute-done.3.twins_ref, bf16[256,256]{1,0:T(8,128)(2,1)S(1)} %bitcast.15, ...), custom_call_target="tpu_custom_call" | custom-call | tf_op jit(solution)/shard_map/pallas_call | solution.py:176
  60.0 0.0 collective-permute-done.10.refs_5_
  60.0 0.0 collective-permute-done.8.refs_3_
  60.0 3.6 %shard_map.42 = f32[12,2,128,128]{3,2,1,0:T(8,128)} custom-call(s32[1]{0:T(128)S(6)} %copy.5.kq_ref, bf16[4,304,256]{2,1,0:T(8,128)(2,1)S(1)} %pad_maximum_fusion.lines_ref, bf16[4,304,256]{2,1,0:T(8,128)(2,1)S(1)} %collective-permute-done.3.twins_ref, bf16[256,256]{1,0:T(8,128)(2,1)S(1)} %collective-permute-done.5.refs_0_, ...), custom_call_target="tpu_custom_call" | custom-call | tf_op jit(solution)/shard_map/pallas_call | solution.py:176
  (6 shorter events, 0.0 us)
Async XLA Ops:
  0.0 0.9 %copy-start = (bf16[1,2,128,256]{3,2,1,0:T(8,128)(2,1)S(1)}, bf16[1,2,128,256]{3,2,1,0:T(8,128)(2,1)}, u32[]{:S(2)}) copy-start(bf16[1,2,128,256]{3,2,1,0:T(8,128)(2,1)} %param.3) | copy-start | bytes 393220
  0.9 0.9 %copy-start.1 = (bf16[96,2,256]{2,1,0:T(2,128)(2,1)S(1)}, bf16[96,2,256]{2,1,0:T(2,128)(2,1)}, u32[]{:S(2)}) copy-start(bf16[96,2,256]{2,1,0:T(2,128)(2,1)} %pot_ref.1) | copy-start | bytes 294916
  1.9 13.6 %collective-permute-start = (bf16[304,256]{1,0:T(8,128)(2,1)S(1)}, bf16[304,256]{1,0:T(8,128)(2,1)S(1)}, u32[]{:S(2)}, u32[]{:S(2)}) collective-permute-start(bf16[304,256]{1,0:T(8,128)(2,1)S(1)} %get-tuple-element.10), channel_id=1, source_target_pairs={{0,2},{2,4},{4,6},{6,0},{1,3},{3,5},{5,7},{7,1},{8,10},{10,12},{12... | collective-permute-start | bytes 466952 | tf_op jit(solution)/shard_map/ppermute | solution.py:194
  4.4 11.1 %collective-permute-start.1 = (bf16[304,256]{1,0:T(8,128)(2,1)S(1)}, bf16[304,256]{1,0:T(8,128)(2,1)S(1)}, u32[]{:S(2)}, u32[]{:S(2)}) collective-permute-start(bf16[304,256]{1,0:T(8,128)(2,1)S(1)} %get-tuple-element.11), channel_id=1, source_target_pairs={{0,6},{2,0},{4,2},{6,4},{1,7},{3,1},{5,3},{7,5},{8,14},{10,8},{12,... | collective-permute-start | bytes 466952 | tf_op jit(solution)/shard_map/ppermute | solution.py:194
  7.2 14.4 %collective-permute-start.2 = (bf16[304,256]{1,0:T(8,128)(2,1)S(1)}, bf16[304,256]{1,0:T(8,128)(2,1)S(1)}, u32[]{:S(2)}, u32[]{:S(2)}) collective-permute-start(bf16[304,256]{1,0:T(8,128)(2,1)S(1)} %get-tuple-element.12), channel_id=1, source_target_pairs={{0,4},{2,6},{4,0},{6,2},{1,5},{3,7},{5,1},{7,3},{8,12},{10,14},{12... | collective-permute-start | bytes 466952 | tf_op jit(solution)/shard_map/ppermute | solution.py:194
  8.8 13.7 %all-to-all-start = ((bf16[16,24,256]{2,1,0:T(8,128)(2,1)}), bf16[16,24,256]{2,1,0:T(8,128)(2,1)S(1)}, u32[]{:S(2)}, u32[]{:S(2)}) async-start(bf16[16,24,256]{2,1,0:T(8,128)(2,1)} %shard_map.38), calls=%async_computation | async-start | bytes 393216 | tf_op jit(solution)/shard_map/all_to_all | solution.py:192
  21.7 37.1 %collective-permute-start.3 = (bf16[4,304,256]{2,1,0:T(8,128)(2,1)S(1)}, bf16[4,304,256]{2,1,0:T(8,128)(2,1)S(1)}, u32[]{:S(2)}, u32[]{:S(2)}) collective-permute-start(bf16[4,304,256]{2,1,0:T(8,128)(2,1)S(1)} %pad_maximum_fusion.lines_ref), channel_id=1, source_target_pairs={{0,1},{1,0},{2,3},{3,2},{4,5},{5,4},{6,7},{7,6},{8,9},{9,8},{10,11... | collective-permute-start | bytes 1867784 | tf_op jit(solution)/shard_map/ppermute | solution.py:196
  22.5 6.1 %collective-permute-start.4 = (bf16[16,16,256]{2,1,0:T(8,128)(2,1)S(1)}, bf16[16,16,256]{2,1,0:T(8,128)(2,1)S(1)}, u32[]{:S(2)}, u32[]{:S(2)}) collective-permute-start(bf16[16,16,256]{2,1,0:T(8,128)(2,1)S(1)} %shard_map.39), channel_id=1, source_target_pairs={{0,134},{2,132},{4,130},{6,128},{128,6},{130,4},{132,2},{134,0},{1... | collective-permute-start | bytes 393224 | tf_op jit(solution)/shard_map/ppermute | solution.py:197
  45.7 5.0 %collective-permute-start.7 = (bf16[256,256]{1,0:T(8,128)(2,1)S(1)}, bf16[256,256]{1,0:T(8,128)(2,1)S(1)}, u32[]{:S(2)}, u32[]{:S(2)}) collective-permute-start(bf16[256,256]{1,0:T(8,128)(2,1)S(1)} %bitcast.11), channel_id=1, source_target_pairs={{0,4},{2,6},{4,0},{6,2},{1,5},{3,7},{5,1},{7,3},{8,12},{10,14},{12... | collective-permute-start | bytes 393224 | tf_op jit(solution)/shard_map/ppermute | solution.py:200
  45.7 12.6 %collective-permute-start.6 = (bf16[256,256]{1,0:T(8,128)(2,1)S(1)}, bf16[256,256]{1,0:T(8,128)(2,1)S(1)}, u32[]{:S(2)}, u32[]{:S(2)}) collective-permute-start(bf16[256,256]{1,0:T(8,128)(2,1)S(1)} %bitcast.12), channel_id=1, source_target_pairs={{0,6},{2,0},{4,2},{6,4},{1,7},{3,1},{5,3},{7,5},{8,14},{10,8},{12,... | collective-permute-start | bytes 393224 | tf_op jit(solution)/shard_map/ppermute | solution.py:200
  46.8 11.5 %collective-permute-start.5 = (bf16[256,256]{1,0:T(8,128)(2,1)S(1)}, bf16[256,256]{1,0:T(8,128)(2,1)S(1)}, u32[]{:S(2)}, u32[]{:S(2)}) collective-permute-start(bf16[256,256]{1,0:T(8,128)(2,1)S(1)} %bitcast.13), channel_id=1, source_target_pairs={{0,2},{2,4},{4,6},{6,0},{1,3},{3,5},{5,7},{7,1},{8,10},{10,12},{12... | collective-permute-start | bytes 393224 | tf_op jit(solution)/shard_map/ppermute | solution.py:200
  47.2 11.7 %collective-permute-start.11 = (bf16[256,256]{1,0:T(8,128)(2,1)S(1)}, bf16[256,256]{1,0:T(8,128)(2,1)S(1)}, u32[]{:S(2)}, u32[]{:S(2)}) collective-permute-start(bf16[256,256]{1,0:T(8,128)(2,1)S(1)} %bitcast.14), channel_id=1, source_target_pairs={{0,1},{1,0},{2,3},{3,2},{4,5},{5,4},{6,7},{7,6},{8,9},{9,8},{10,11... | collective-permute-start | bytes 393224 | tf_op jit(solution)/shard_map/ppermute | solution.py:201
  50.7 9.3 %collective-permute-start.10 = (bf16[256,256]{1,0:T(8,128)(2,1)S(1)}, bf16[256,256]{1,0:T(8,128)(2,1)S(1)}, u32[]{:S(2)}, u32[]{:S(2)}) collective-permute-start(bf16[256,256]{1,0:T(8,128)(2,1)S(1)} %collective-permute-done.7.refs_2_), channel_id=1, source_target_pairs={{0,1},{1,0},{2,3},{3,2},{4,5},{5,4},{6,7},{7,6},{8,9},{9,8},{10,11... | collective-permute-start | bytes 393224 | tf_op jit(solution)/shard_map/ppermute | solution.py:201
  58.3 1.6 %collective-permute-start.9 = (bf16[256,256]{1,0:T(8,128)(2,1)S(1)}, bf16[256,256]{1,0:T(8,128)(2,1)S(1)}, u32[]{:S(2)}, u32[]{:S(2)}) collective-permute-start(bf16[256,256]{1,0:T(8,128)(2,1)S(1)} %collective-permute-done.6.refs_1_), channel_id=1, source_target_pairs={{0,1},{1,0},{2,3},{3,2},{4,5},{5,4},{6,7},{7,6},{8,9},{9,8},{10,11... | collective-permute-start | bytes 393224 | tf_op jit(solution)/shard_map/ppermute | solution.py:201
  58.3 1.6 %collective-permute-start.8 = (bf16[256,256]{1,0:T(8,128)(2,1)S(1)}, bf16[256,256]{1,0:T(8,128)(2,1)S(1)}, u32[]{:S(2)}, u32[]{:S(2)}) collective-permute-start(bf16[256,256]{1,0:T(8,128)(2,1)S(1)} %collective-permute-done.5.refs_0_), channel_id=1, source_target_pairs={{0,1},{1,0},{2,3},{3,2},{4,5},{5,4},{6,7},{7,6},{8,9},{9,8},{10,11... | collective-permute-start | bytes 393224 | tf_op jit(solution)/shard_map/ppermute | solution.py:201
where the time goes:
time: 64 us; the launch traced here: 63.7 us
  starting transfers between devices  29.2 us (46%)
  blocking collectives  16.9 us (26%)
  waiting for transfers between devices  9.19 us (14%)
  Pallas kernels  5.72 us (9%)
  local copies, waits for them, and re-layouts  1.8 us (3%)
  between operations  0.9 us (1%)
    all_to_all x1, blocking collectives, body(): lax.all_to_all(choose(tagged, swapped), XY, 0, 0, tiled=True)  16.9 us
    ppermute x4, starting transfers between devices, body(): mates = [lax.ppermute(o, 'c', SWAP) for o in others]  11.1 us
    all_to_all x1, starting transfers between devices, body(): tagged = lax.all_to_all(tagged, XY, 0, 0, tiled=True)  6.75 us
    ppermute x3, waiting for transfers between devices, body(): lax.ppermute(packs[i], 'zl', ring(STEPS[i]))  6.08 us
    ppermute x3, starting transfers between devices, body(): lax.ppermute(packs[i], 'zl', ring(STEPS[i]))  5.53 us
    pallas_call x2, Pallas kernels, couple(): pl.pallas_call(kernel, in_specs=specs, out_specs=pl.BlockSpec(memory_spac...  4.66 us
    ppermute x1, starting transfers between devices, body(): swapped = lax.ppermute(strip(tagged), ('zh', 'zl'), MIRROR)  3.77 us
    ppermute x1, waiting for transfers between devices, body(): swapped = lax.ppermute(strip(tagged), ('zh', 'zl'), MIRROR)  2.36 us
  transfers between devices with their start and end apart: 13, of which 4 were waited for; matrix products, arithmetic and copies ran while one was open for 0% of the time, Pallas kernels for 3%

commit v1 on v0

--- a/solution.py
+++ b/solution.py
@@ -15,6 +15,7 @@
 TAG = 8
 SMALL = pltpu.CompilerParams(vmem_limit_bytes=20 * 2**20)
 IN_SMEM = pl.BlockSpec(memory_space=pltpu.SMEM)
+IN_HBM = pl.BlockSpec(memory_space=pltpu.HBM)
 IN_VMEM = pl.BlockSpec(memory_space=pltpu.VMEM)
 
 
@@ -46,18 +47,22 @@
     rows, cells = slab.shape
     piece = rows // 16
 
-    def kernel(kq_ref, slab_ref, out):
-        tag = jnp.full((TAG, cells), kq_ref[0].astype(jnp.float32)).astype(slab.dtype)
-        for j in range(16):
-            out[j, :piece] = slab_ref[j * piece : (j + 1) * piece]
-            out[j, piece:] = tag
-
-    return pl.pallas_call(
-        kernel,
-        in_specs=[IN_SMEM, IN_VMEM],
+    def kernel(kq_ref, slab_ref, out, tags, sems):
+        body = pltpu.make_async_copy(slab_ref, out.at[:, :piece], sems.at[0])
+        body.start()
+        tags[...] = jnp.full(tags.shape, kq_ref[0].astype(jnp.float32)).astype(slab.dtype)
+        tail = pltpu.make_async_copy(tags, out.at[:, piece:], sems.at[1])
+        tail.start()
+        body.wait()
+        tail.wait()
+
+    return pl.pallas_call(
+        kernel,
+        in_specs=[IN_SMEM, IN_HBM],
+        out_specs=IN_HBM,
         out_shape=jax.ShapeDtypeStruct((16, piece + TAG, cells), slab.dtype),
-        compiler_params=SMALL,
-    )(kq, slab)
+        scratch_shapes=[pltpu.VMEM((16, TAG, cells), slab.dtype), pltpu.SemaphoreType.DMA((2,))],
+    )(kq, slab.reshape(16, piece, cells))
 
 
 def strip(tagged):
@@ -176,7 +181,7 @@
     return pl.pallas_call(
         kernel,
         in_specs=specs,
-        out_specs=pl.BlockSpec(memory_space=pl.ANY) if last else IN_VMEM,
+        out_specs=IN_HBM if last else IN_VMEM,
         out_shape=jax.ShapeDtypeStruct(total, jnp.float32),
         scratch_shapes=scratch,
         compiler_params=SMALL,

time: 64 us -> 66.3 us (1.036)
  blocking collectives: 16.9 us -> 10.1 us
  starting transfers between devices: 29.2 us -> 34.4 us
  Pallas kernels: 5.72 us -> 10.1 us
    all_to_all x1, blocking collectives: 16.9 us -> 10.1 us  [body(): lax.all_to_all(choose(tagged, swapped), XY, 0, 0, tiled=True)]
    all_to_all x1, waiting for transfers between devices: 0.16 us -> 4.58 us  [body(): tagged = lax.all_to_all(tagged, XY, 0, 0, tiled=True)]
    ppermute x3, waiting for transfers between devices: 6.08 us -> 1.66 us  [body(): lax.ppermute(packs[i], 'zl', ring(STEPS[i]))]
    pallas_call x3, Pallas kernels: 5.35 us -> 9.76 us  [the longest x1 5.09 us: pack_spread(): pl.pallas_call(kernel, in_specs=[IN_SMEM, IN_HBM], out_specs=IN_HBM, out_...]
    ppermute x3, starting transfers between devices: 1.47 us -> 5.6 us  [body(): lax.ppermute(phi, 'zl', ring(STEPS[i]))]
    ppermute x4, starting transfers between devices: 11.1 us -> 12.2 us  [body(): mates = [lax.ppermute(o, 'c', SWAP) for o in others]]
  transfers between devices with their start and end apart: 13 -> 13, of which waited for: 4 -> 3; matrix products, arithmetic and copies ran while one was open for 0% -> 0% of each run, Pallas kernels for 3% -> 10%
where the time goes in v1:
time: 66.3 us; the launch traced here: 66.1 us
  starting transfers between devices  34.4 us (52%)
  Pallas kernels  10.1 us (15%)
  blocking collectives  10.1 us (15%)
  waiting for transfers between devices  8.63 us (13%)
  local copies, waits for them, and re-layouts  1.8 us (3%)
  between operations  0.91 us (1%)
    ppermute x4, starting transfers between devices, body(): mates = [lax.ppermute(o, 'c', SWAP) for o in others]  12.2 us
    all_to_all x1, blocking collectives, body(): lax.all_to_all(choose(tagged, swapped), XY, 0, 0, tiled=True)  10.1 us
    all_to_all x1, starting transfers between devices, body(): tagged = lax.all_to_all(tagged, XY, 0, 0, tiled=True)  6.77 us
    ppermute x3, starting transfers between devices, body(): lax.ppermute(phi, 'zl', ring(STEPS[i]))  5.6 us
    ppermute x3, starting transfers between devices, body(): lax.ppermute(packs[i], 'zl', ring(STEPS[i]))  5.53 us
    pallas_call x1, Pallas kernels, pack_spread(): pl.pallas_call(kernel, in_specs=[IN_SMEM, IN_HBM], out_specs=IN_HBM, out_...  5.09 us
    pallas_call x2, Pallas kernels, couple(): pl.pallas_call(kernel, in_specs=specs, out_specs=IN_HBM if last else IN_V...  4.67 us
    all_to_all x1, waiting for transfers between devices, body(): tagged = lax.all_to_all(tagged, XY, 0, 0, tiled=True)  4.58 us
  transfers between devices with their start and end apart: 13, of which 3 were waited for; matrix products, arithmetic and copies ran while one was open for 0% of the time, Pallas kernels for 10%

profile of v1, /device:TPU:1, one launch (start us, length us, event | category | flops | bytes accessed | tf_op | source)
XLA Modules:
  0.0 66.1 jit_solution(8050438493605034074)
XLA Ops:
  0.0 0.9 %copy-done = bf16[1,2,128,256]{3,2,1,0:T(8,128)(2,1)S(1)} copy-done((bf16[1,2,128,256]{3,2,1,0:T(8,128)(2,1)S(1)}, bf16[1,2,128,256]{3,2,1,0:T(8,128)(2,1)}, u32[]{:S(2)}) %copy-start) | copy-done | bytes 131096
  0.9 0.9 %copy-done.1 = bf16[96,2,256]{2,1,0:T(2,128)(2,1)S(1)} copy-done((bf16[96,2,256]{2,1,0:T(2,128)(2,1)S(1)}, bf16[96,2,256]{2,1,0:T(2,128)(2,1)}, u32[]{:S(2)}) %copy-start.1) | copy-done | bytes 98328
  1.8 0.1 shard_map.37
  1.9 2.5 %collective-permute-start = (bf16[304,256]{1,0:T(8,128)(2,1)S(1)}, bf16[304,256]{1,0:T(8,128)(2,1)S(1)}, u32[]{:S(2)}, u32[]{:S(2)}) collective-permute-start(bf16[304,256]{1,0:T(8,128)(2,1)S(1)} %get-tuple-element.10), channel_id=1, source_target_pairs={{0,2},{2,4},{4,6},{6,0},{1,3},{3,5},{5,7},{7,1},{8,10},{10,12},{12... | collective-permute-start | bytes 466952 | tf_op jit(solution)/shard_map/ppermute | solution.py:199
  4.4 2.8 %collective-permute-start.1 = (bf16[304,256]{1,0:T(8,128)(2,1)S(1)}, bf16[304,256]{1,0:T(8,128)(2,1)S(1)}, u32[]{:S(2)}, u32[]{:S(2)}) collective-permute-start(bf16[304,256]{1,0:T(8,128)(2,1)S(1)} %get-tuple-element.11), channel_id=1, source_target_pairs={{0,6},{2,0},{4,2},{6,4},{1,7},{3,1},{5,3},{7,5},{8,14},{10,8},{12,... | collective-permute-start | bytes 466952 | tf_op jit(solution)/shard_map/ppermute | solution.py:199
  7.2 0.2 collective-permute-start.2
  8.1 5.1 %shard_map.38 = bf16[16,24,256]{2,1,0:T(8,128)(2,1)} custom-call(s32[1]{0:T(128)S(6)} %copy.5.kq_ref, bf16[16,16,256]{2,1,0:T(8,128)(2,1)} %bitcast.10), custom_call_target="tpu_custom_call" | custom-call | tf_op jit(solution)/shard_map/pallas_call | solution.py:59
  13.2 6.8 %all-to-all-start = ((bf16[16,24,256]{2,1,0:T(8,128)(2,1)}), bf16[16,24,256]{2,1,0:T(8,128)(2,1)S(1)}, u32[]{:S(2)}, u32[]{:S(2)}) async-start(bf16[16,24,256]{2,1,0:T(8,128)(2,1)} %shard_map.38), calls=%async_computation | async-start | bytes 393216 | tf_op jit(solution)/shard_map/all_to_all | solution.py:197
  20.0 0.0 collective-permute-done
  20.0 0.0 collective-permute-done.1
  20.0 1.7 %collective-permute-done.2 = bf16[304,256]{1,0:T(8,128)(2,1)S(1)} collective-permute-done((bf16[304,256]{1,0:T(8,128)(2,1)S(1)}, bf16[304,256]{1,0:T(8,128)(2,1)S(1)}, u32[]{:S(2)}, u32[]{:S(2)}) %collective-permute-start.2) | collective-permute-done | bytes 155680 | tf_op jit(solution)/shard_map/ppermute | solution.py:199
  21.6 0.1 pad_maximum_fusion.lines_ref
  21.7 0.6 collective-permute-start.3
  22.3 4.6 %all-to-all-done.ref = bf16[16,24,256]{2,1,0:T(8,128)(2,1)S(1)} async-done(((bf16[16,24,256]{2,1,0:T(8,128)(2,1)}), bf16[16,24,256]{2,1,0:T(8,128)(2,1)S(1)}, u32[]{:S(2)}, u32[]{:S(2)}) %all-to-all-start) | async-done | bytes 196640 | tf_op jit(solution)/shard_map/all_to_all | solution.py:197
  26.9 3.8 %collective-permute-start.4 = (bf16[16,16,256]{2,1,0:T(8,128)(2,1)S(1)}, bf16[16,16,256]{2,1,0:T(8,128)(2,1)S(1)}, u32[]{:S(2)}, u32[]{:S(2)}) collective-permute-start(bf16[16,16,256]{2,1,0:T(8,128)(2,1)S(1)} %shard_map.39), channel_id=1, source_target_pairs={{0,134},{2,132},{4,130},{6,128},{128,6},{130,4},{132,2},{134,0},{1... | collective-permute-start | bytes 393224 | tf_op jit(solution)/shard_map/ppermute | solution.py:202
  30.7 2.4 %collective-permute-done.4.swapped_ref = bf16[16,16,256]{2,1,0:T(8,128)(2,1)S(1)} collective-permute-done((bf16[16,16,256]{2,1,0:T(8,128)(2,1)S(1)}, bf16[16,16,256]{2,1,0:T(8,128)(2,1)S(1)}, u32[]{:S(2)}, u32[]{:S(2)}) %collective-permute-start.4) | collective-permute-done | bytes 131104 | tf_op jit(solution)/shard_map/ppermute | solution.py:202
  33.0 0.2 shard_map.40
  33.3 10.1 %all_to_all.10 = bf16[16,16,256]{2,1,0:T(8,128)(2,1)S(1)} all-to-all(bf16[16,16,256]{2,1,0:T(8,128)(2,1)S(1)} %shard_map.40), channel_id=1, replica_groups=mesh['zh'=2,'x'=4,'y'=4,'zl'=4,'c'=2] {'x','y'}, dimensions={0} | all-to-all | bytes 262144 | tf_op jit(solution)/shard_map/all_to_all | solution.py:203
  43.4 3.2 %collective-permute-start.7 = (bf16[256,256]{1,0:T(8,128)(2,1)S(1)}, bf16[256,256]{1,0:T(8,128)(2,1)S(1)}, u32[]{:S(2)}, u32[]{:S(2)}) collective-permute-start(bf16[256,256]{1,0:T(8,128)(2,1)S(1)} %bitcast.12), channel_id=1, source_target_pairs={{0,4},{2,6},{4,0},{6,2},{1,5},{3,7},{5,1},{7,3},{8,12},{10,14},{12... | collective-permute-start | bytes 393224 | tf_op jit(solution)/shard_map/ppermute | solution.py:205
  46.6 2.4 %collective-permute-start.6 = (bf16[256,256]{1,0:T(8,128)(2,1)S(1)}, bf16[256,256]{1,0:T(8,128)(2,1)S(1)}, u32[]{:S(2)}, u32[]{:S(2)}) collective-permute-start(bf16[256,256]{1,0:T(8,128)(2,1)S(1)} %bitcast.13), channel_id=1, source_target_pairs={{0,6},{2,0},{4,2},{6,4},{1,7},{3,1},{5,3},{7,5},{8,14},{10,8},{12,... | collective-permute-start | bytes 393224 | tf_op jit(solution)/shard_map/ppermute | solution.py:205
  49.0 0.0 collective-permute-start.5
  49.0 5.4 %collective-permute-start.11 = (bf16[256,256]{1,0:T(8,128)(2,1)S(1)}, bf16[256,256]{1,0:T(8,128)(2,1)S(1)}, u32[]{:S(2)}, u32[]{:S(2)}) collective-permute-start(bf16[256,256]{1,0:T(8,128)(2,1)S(1)} %bitcast.15), channel_id=1, source_target_pairs={{0,1},{1,0},{2,3},{3,2},{4,5},{5,4},{6,7},{7,6},{8,9},{9,8},{10,11... | collective-permute-start | bytes 393224 | tf_op jit(solution)/shard_map/ppermute | solution.py:206
  54.4 0.0 collective-permute-done.7.refs_2_
  54.4 3.5 %collective-permute-start.10 = (bf16[256,256]{1,0:T(8,128)(2,1)S(1)}, bf16[256,256]{1,0:T(8,128)(2,1)S(1)}, u32[]{:S(2)}, u32[]{:S(2)}) collective-permute-start(bf16[256,256]{1,0:T(8,128)(2,1)S(1)} %collective-permute-done.7.refs_2_), channel_id=1, source_target_pairs={{0,1},{1,0},{2,3},{3,2},{4,5},{5,4},{6,7},{7,6},{8,9},{9,8},{10,11... | collective-permute-start | bytes 393224 | tf_op jit(solution)/shard_map/ppermute | solution.py:206
  58.0 0.0 collective-permute-done.6.refs_1_
  58.0 0.0 collective-permute-start.9
  58.0 0.0 collective-permute-done.5.refs_0_
  58.0 3.2 %collective-permute-start.8 = (bf16[256,256]{1,0:T(8,128)(2,1)S(1)}, bf16[256,256]{1,0:T(8,128)(2,1)S(1)}, u32[]{:S(2)}, u32[]{:S(2)}) collective-permute-start(bf16[256,256]{1,0:T(8,128)(2,1)S(1)} %collective-permute-done.5.refs_0_), channel_id=1, source_target_pairs={{0,1},{1,0},{2,3},{3,2},{4,5},{5,4},{6,7},{7,6},{8,9},{9,8},{10,11... | collective-permute-start | bytes 393224 | tf_op jit(solution)/shard_map/ppermute | solution.py:206
  61.2 1.1 %shard_map.41.refs_6_ = f32[12,2,128,128]{3,2,1,0:T(8,128)S(1)} custom-call(s32[1]{0:T(128)S(6)} %copy.5.kq_ref, bf16[4,304,256]{2,1,0:T(8,128)(2,1)S(1)} %pad_maximum_fusion.lines_ref, bf16[4,304,256]{2,1,0:T(8,128)(2,1)S(1)} %collective-permute-done.3.twins_ref, bf16[256,256]{1,0:T(8,128)(2,1)S(1)} %bitcast.16, ...), custom_call_target="tpu_custom_call" | custom-call | tf_op jit(solution)/shard_map/pallas_call | solution.py:181
  62.3 0.0 collective-permute-done.9.refs_4_
  62.3 0.0 collective-permute-done.8.refs_3_
  62.3 3.6 %shard_map.42 = f32[12,2,128,128]{3,2,1,0:T(8,128)} custom-call(s32[1]{0:T(128)S(6)} %copy.5.kq_ref, bf16[4,304,256]{2,1,0:T(8,128)(2,1)S(1)} %pad_maximum_fusion.lines_ref, bf16[4,304,256]{2,1,0:T(8,128)(2,1)S(1)} %collective-permute-done.3.twins_ref, bf16[256,256]{1,0:T(8,128)(2,1)S(1)} %collective-permute-done.5.refs_0_, ...), custom_call_target="tpu_custom_call" | custom-call | tf_op jit(solution)/shard_map/pallas_call | solution.py:181
  (6 shorter events, 0.0 us)
Async XLA Ops:
  0.0 0.9 %copy-start = (bf16[1,2,128,256]{3,2,1,0:T(8,128)(2,1)S(1)}, bf16[1,2,128,256]{3,2,1,0:T(8,128)(2,1)}, u32[]{:S(2)}) copy-start(bf16[1,2,128,256]{3,2,1,0:T(8,128)(2,1)} %param.3) | copy-start | bytes 393220
  0.9 0.9 %copy-start.1 = (bf16[96,2,256]{2,1,0:T(2,128)(2,1)S(1)}, bf16[96,2,256]{2,1,0:T(2,128)(2,1)}, u32[]{:S(2)}) copy-start(bf16[96,2,256]{2,1,0:T(2,128)(2,1)} %pot_ref.1) | copy-start | bytes 294916
  1.9 18.1 %collective-permute-start = (bf16[304,256]{1,0:T(8,128)(2,1)S(1)}, bf16[304,256]{1,0:T(8,128)(2,1)S(1)}, u32[]{:S(2)}, u32[]{:S(2)}) collective-permute-start(bf16[304,256]{1,0:T(8,128)(2,1)S(1)} %get-tuple-element.10), channel_id=1, source_target_pairs={{0,2},{2,4},{4,6},{6,0},{1,3},{3,5},{5,7},{7,1},{8,10},{10,12},{12... | collective-permute-start | bytes 466952 | tf_op jit(solution)/shard_map/ppermute | solution.py:199
  4.4 15.5 %collective-permute-start.1 = (bf16[304,256]{1,0:T(8,128)(2,1)S(1)}, bf16[304,256]{1,0:T(8,128)(2,1)S(1)}, u32[]{:S(2)}, u32[]{:S(2)}) collective-permute-start(bf16[304,256]{1,0:T(8,128)(2,1)S(1)} %get-tuple-element.11), channel_id=1, source_target_pairs={{0,6},{2,0},{4,2},{6,4},{1,7},{3,1},{5,3},{7,5},{8,14},{10,8},{12,... | collective-permute-start | bytes 466952 | tf_op jit(solution)/shard_map/ppermute | solution.py:199
  7.2 14.4 %collective-permute-start.2 = (bf16[304,256]{1,0:T(8,128)(2,1)S(1)}, bf16[304,256]{1,0:T(8,128)(2,1)S(1)}, u32[]{:S(2)}, u32[]{:S(2)}) collective-permute-start(bf16[304,256]{1,0:T(8,128)(2,1)S(1)} %get-tuple-element.12), channel_id=1, source_target_pairs={{0,4},{2,6},{4,0},{6,2},{1,5},{3,7},{5,1},{7,3},{8,12},{10,14},{12... | collective-permute-start | bytes 466952 | tf_op jit(solution)/shard_map/ppermute | solution.py:199
  13.2 13.7 %all-to-all-start = ((bf16[16,24,256]{2,1,0:T(8,128)(2,1)}), bf16[16,24,256]{2,1,0:T(8,128)(2,1)S(1)}, u32[]{:S(2)}, u32[]{:S(2)}) async-start(bf16[16,24,256]{2,1,0:T(8,128)(2,1)} %shard_map.38), calls=%async_computation | async-start | bytes 393216 | tf_op jit(solution)/shard_map/all_to_all | solution.py:197
  21.7 39.5 %collective-permute-start.3 = (bf16[4,304,256]{2,1,0:T(8,128)(2,1)S(1)}, bf16[4,304,256]{2,1,0:T(8,128)(2,1)S(1)}, u32[]{:S(2)}, u32[]{:S(2)}) collective-permute-start(bf16[4,304,256]{2,1,0:T(8,128)(2,1)S(1)} %pad_maximum_fusion.lines_ref), channel_id=1, source_target_pairs={{0,1},{1,0},{2,3},{3,2},{4,5},{5,4},{6,7},{7,6},{8,9},{9,8},{10,11... | collective-permute-start | bytes 1867784 | tf_op jit(solution)/shard_map/ppermute | solution.py:201
  26.9 6.1 %collective-permute-start.4 = (bf16[16,16,256]{2,1,0:T(8,128)(2,1)S(1)}, bf16[16,16,256]{2,1,0:T(8,128)(2,1)S(1)}, u32[]{:S(2)}, u32[]{:S(2)}) collective-permute-start(bf16[16,16,256]{2,1,0:T(8,128)(2,1)S(1)} %shard_map.39), channel_id=1, source_target_pairs={{0,134},{2,132},{4,130},{6,128},{128,6},{130,4},{132,2},{134,0},{1... | collective-permute-start | bytes 393224 | tf_op jit(solution)/shard_map/ppermute | solution.py:202
  43.4 11.0 %collective-permute-start.7 = (bf16[256,256]{1,0:T(8,128)(2,1)S(1)}, bf16[256,256]{1,0:T(8,128)(2,1)S(1)}, u32[]{:S(2)}, u32[]{:S(2)}) collective-permute-start(bf16[256,256]{1,0:T(8,128)(2,1)S(1)} %bitcast.12), channel_id=1, source_target_pairs={{0,4},{2,6},{4,0},{6,2},{1,5},{3,7},{5,1},{7,3},{8,12},{10,14},{12... | collective-permute-start | bytes 393224 | tf_op jit(solution)/shard_map/ppermute | solution.py:205
  46.6 11.4 %collective-permute-start.6 = (bf16[256,256]{1,0:T(8,128)(2,1)S(1)}, bf16[256,256]{1,0:T(8,128)(2,1)S(1)}, u32[]{:S(2)}, u32[]{:S(2)}) collective-permute-start(bf16[256,256]{1,0:T(8,128)(2,1)S(1)} %bitcast.13), channel_id=1, source_target_pairs={{0,6},{2,0},{4,2},{6,4},{1,7},{3,1},{5,3},{7,5},{8,14},{10,8},{12,... | collective-permute-start | bytes 393224 | tf_op jit(solution)/shard_map/ppermute | solution.py:205
  49.0 9.0 %collective-permute-start.5 = (bf16[256,256]{1,0:T(8,128)(2,1)S(1)}, bf16[256,256]{1,0:T(8,128)(2,1)S(1)}, u32[]{:S(2)}, u32[]{:S(2)}) collective-permute-start(bf16[256,256]{1,0:T(8,128)(2,1)S(1)} %bitcast.14), channel_id=1, source_target_pairs={{0,2},{2,4},{4,6},{6,0},{1,3},{3,5},{5,7},{7,1},{8,10},{10,12},{12... | collective-permute-start | bytes 393224 | tf_op jit(solution)/shard_map/ppermute | solution.py:205
  49.0 12.2 %collective-permute-start.11 = (bf16[256,256]{1,0:T(8,128)(2,1)S(1)}, bf16[256,256]{1,0:T(8,128)(2,1)S(1)}, u32[]{:S(2)}, u32[]{:S(2)}) collective-permute-start(bf16[256,256]{1,0:T(8,128)(2,1)S(1)} %bitcast.15), channel_id=1, source_target_pairs={{0,1},{1,0},{2,3},{3,2},{4,5},{5,4},{6,7},{7,6},{8,9},{9,8},{10,11... | collective-permute-start | bytes 393224 | tf_op jit(solution)/shard_map/ppermute | solution.py:206
  54.4 7.9 %collective-permute-start.10 = (bf16[256,256]{1,0:T(8,128)(2,1)S(1)}, bf16[256,256]{1,0:T(8,128)(2,1)S(1)}, u32[]{:S(2)}, u32[]{:S(2)}) collective-permute-start(bf16[256,256]{1,0:T(8,128)(2,1)S(1)} %collective-permute-done.7.refs_2_), channel_id=1, source_target_pairs={{0,1},{1,0},{2,3},{3,2},{4,5},{5,4},{6,7},{7,6},{8,9},{9,8},{10,11... | collective-permute-start | bytes 393224 | tf_op jit(solution)/shard_map/ppermute | solution.py:206
  58.0 4.3 %collective-permute-start.9 = (bf16[256,256]{1,0:T(8,128)(2,1)S(1)}, bf16[256,256]{1,0:T(8,128)(2,1)S(1)}, u32[]{:S(2)}, u32[]{:S(2)}) collective-permute-start(bf16[256,256]{1,0:T(8,128)(2,1)S(1)} %collective-permute-done.6.refs_1_), channel_id=1, source_target_pairs={{0,1},{1,0},{2,3},{3,2},{4,5},{5,4},{6,7},{7,6},{8,9},{9,8},{10,11... | collective-permute-start | bytes 393224 | tf_op jit(solution)/shard_map/ppermute | solution.py:206
  58.0 4.4 %collective-permute-start.8 = (bf16[256,256]{1,0:T(8,128)(2,1)S(1)}, bf16[256,256]{1,0:T(8,128)(2,1)S(1)}, u32[]{:S(2)}, u32[]{:S(2)}) collective-permute-start(bf16[256,256]{1,0:T(8,128)(2,1)S(1)} %collective-permute-done.5.refs_0_), channel_id=1, source_target_pairs={{0,1},{1,0},{2,3},{3,2},{4,5},{5,4},{6,7},{7,6},{8,9},{9,8},{10,11... | collective-permute-start | bytes 393224 | tf_op jit(solution)/shard_map/ppermute | solution.py:206

commit v2 on v0

--- a/solution.py
+++ b/solution.py
@@ -42,54 +42,42 @@
     )(slab, potential)
 
 
-def pack_spread(slab, kq):
+def pack_spread(slab, swapped, kq):
     rows, cells = slab.shape
     piece = rows // 16
 
-    def kernel(kq_ref, slab_ref, out):
+    def kernel(kq_ref, slab_ref, swapped_ref, out):
         tag = jnp.full((TAG, cells), kq_ref[0].astype(jnp.float32)).astype(slab.dtype)
         for j in range(16):
             out[j, :piece] = slab_ref[j * piece : (j + 1) * piece]
-            out[j, piece:] = tag
+            out[j, piece : 2 * piece] = swapped_ref[j * piece : (j + 1) * piece]
+            out[j, 2 * piece :] = tag
 
     return pl.pallas_call(
         kernel,
-        in_specs=[IN_SMEM, IN_VMEM],
-        out_shape=jax.ShapeDtypeStruct((16, piece + TAG, cells), slab.dtype),
+        in_specs=[IN_SMEM, IN_VMEM, IN_VMEM],
+        out_shape=jax.ShapeDtypeStruct((16, 2 * piece + TAG, cells), slab.dtype),
         compiler_params=SMALL,
-    )(kq, slab)
+    )(kq, slab, swapped)
 
 
-def strip(tagged):
-    count, rows, cells = tagged.shape
+def choose(pieces):
+    count, rows, cells = pieces.shape
+    piece = (rows - TAG) // 2
 
     def kernel(ref, out):
-        out[...] = ref[:, : rows - TAG]
+        zh = lax.axis_index("zh")
+        for d in range(count):
+            source = jnp.max(ref[d, 2 * piece :, :128].astype(jnp.float32)).astype(jnp.int32)
+            side = jnp.where(source // count == zh, 0, piece)
+            out[d] = ref[lax.rem(source, count), pl.ds(pl.multiple_of(side, piece), piece), :]
 
     return pl.pallas_call(
         kernel,
         in_specs=[IN_VMEM],
-        out_shape=jax.ShapeDtypeStruct((count, rows - TAG, cells), tagged.dtype),
+        out_shape=jax.ShapeDtypeStruct((count, piece, cells), pieces.dtype),
         compiler_params=SMALL,
-    )(tagged)
-
-
-def choose(tagged, swapped):
-    count, piece, _ = swapped.shape
-
-    def kernel(ref, swapped_ref, out):
-        zh = lax.axis_index("zh")
-        for d in range(count):
-            source = jnp.max(ref[d, piece:, :128].astype(jnp.float32)).astype(jnp.int32)
-            block = lax.rem(source, count)
-            out[d] = jnp.where(source // count == zh, ref[block, :piece], swapped_ref[block])
-
-    return pl.pallas_call(
-        kernel,
-        in_specs=[IN_VMEM, IN_VMEM],
-        out_shape=jax.ShapeDtypeStruct(swapped.shape, swapped.dtype),
-        compiler_params=SMALL,
-    )(tagged, swapped)
+    )(pieces)
 
 
 def couple(kq, lines, twins, others, steps, bands, modes, last, before=None):
@@ -188,19 +176,19 @@
     modes = dvscf.shape[0] // 8
     slab = psi.reshape(2 * bands, cells)
 
-    tagged = pack_spread(slab, kq_map)
-    tagged = lax.all_to_all(tagged, XY, 0, 0, tiled=True)
+    swapped = lax.ppermute(slab, ("zh", "zl"), MIRROR)
     packs = pack_lines(slab, dvscf)
+    pieces = lax.all_to_all(pack_spread(slab, swapped, kq_map), XY, 0, 0, tiled=True)
     lines = [packs[0]] + [lax.ppermute(packs[i], "zl", ring(STEPS[i])) for i in (1, 2, 3)]
     lines = jnp.stack(lines)
     twins = lax.ppermute(lines, "c", SWAP)
-    swapped = lax.ppermute(strip(tagged), ("zh", "zl"), MIRROR)
-    phi = lax.all_to_all(choose(tagged, swapped), XY, 0, 0, tiled=True).reshape(2 * bands, cells)
+    phi = lax.all_to_all(choose(pieces), XY, 0, 0, tiled=True).reshape(2 * bands, cells)
 
     others = [phi] + [lax.ppermute(phi, "zl", ring(STEPS[i])) for i in (1, 2, 3)]
     mates = [lax.ppermute(o, "c", SWAP) for o in others]
-    out = couple(kq_map, lines, twins, others[:1] + mates[:1], STEPS[:1], bands, modes, False)
-    out = couple(kq_map, lines, twins, others[1:] + mates[1:], STEPS[1:], bands, modes, True, out)
+    out = None
+    for name, at in (("early", slice(0, 1)), ("middle", slice(1, 3)), ("late", slice(3, 4))):
+        out = couple(kq_map, lines, twins, others[at] + mates[at], STEPS[at], bands, modes, name == "late", out)
     return out[:, None]
 
 

time: 64 us -> 70.2 us (1.097)
  starting transfers between devices: 29.2 us -> 40.8 us
  blocking collectives: 16.9 us -> 10.2 us
  waiting for transfers between devices: 9.19 us -> 10.1 us
    ppermute x3, starting transfers between devices: 1.47 us -> 12.9 us  [body(): lax.ppermute(phi, 'zl', ring(STEPS[i]))]
    all_to_all x1, blocking collectives: 16.9 us -> 10.2 us  [body(): lax.all_to_all(choose(pieces), XY, 0, 0, tiled=True)]
    ppermute x3, waiting for transfers between devices: 6.08 us -> 0.78 us  [body(): lax.ppermute(packs[i], 'zl', ring(STEPS[i]))]
    all_to_all x1, waiting for transfers between devices: 0.16 us -> 4.72 us  [body(): lax.all_to_all(pack_spread(slab, swapped, kq_map), XY, 0, 0, tiled=True)]
    ppermute x3, waiting for transfers between devices: 0.58 us -> 2.77 us  [body(): lax.ppermute(phi, 'zl', ring(STEPS[i]))]
    ppermute x1, starting transfers between devices: 0.58 us -> 2.09 us  [body(): twins = lax.ppermute(lines, 'c', SWAP)]
    ppermute x4, starting transfers between devices: 11.1 us -> 10.1 us  [body(): mates = [lax.ppermute(o, 'c', SWAP) for o in others]]
    pallas_call x2 -> x3, Pallas kernels: 4.66 us -> 4.99 us  [couple(): pl.pallas_call(kernel, in_specs=specs, out_specs=pl.BlockSpec(memory_spac...]
  transfers between devices with their start and end apart: 13 -> 13, of which waited for: 4 -> 4; matrix products, arithmetic and copies ran while one was open for 0% -> 0% of each run, Pallas kernels for 3% -> 6%
where the time goes in v2:
time: 70.2 us; the launch traced here: 70 us
  starting transfers between devices  40.8 us (58%)
  blocking collectives  10.2 us (15%)
  waiting for transfers between devices  10.1 us (14%)
  Pallas kernels  6.1 us (9%)
  local copies, waits for them, and re-layouts  1.8 us (3%)
  between operations  0.9 us (1%)
    ppermute x3, starting transfers between devices, body(): lax.ppermute(phi, 'zl', ring(STEPS[i]))  12.9 us
    all_to_all x1, blocking collectives, body(): lax.all_to_all(choose(pieces), XY, 0, 0, tiled=True)  10.2 us
    ppermute x4, starting transfers between devices, body(): mates = [lax.ppermute(o, 'c', SWAP) for o in others]  10.1 us
    all_to_all x1, starting transfers between devices, body(): lax.all_to_all(pack_spread(slab, swapped, kq_map), XY, 0, 0, tiled=True)  6.64 us
    ppermute x3, starting transfers between devices, body(): lax.ppermute(packs[i], 'zl', ring(STEPS[i]))  5.53 us
    pallas_call x3, Pallas kernels, couple(): pl.pallas_call(kernel, in_specs=specs, out_specs=pl.BlockSpec(memory_spac...  4.99 us
    all_to_all x1, waiting for transfers between devices, body(): lax.all_to_all(pack_spread(slab, swapped, kq_map), XY, 0, 0, tiled=True)  4.72 us
    ppermute x1, starting transfers between devices, body(): swapped = lax.ppermute(slab, ('zh', 'zl'), MIRROR)  3.58 us
  transfers between devices with their start and end apart: 13, of which 4 were waited for; matrix products, arithmetic and copies ran while one was open for 0% of the time, Pallas kernels for 6%

profile of v2, /device:TPU:1, one launch (start us, length us, event | category | flops | bytes accessed | tf_op | source)
XLA Modules:
  0.0 70.0 jit_solution(10009363145387781182)
XLA Ops:
  0.0 0.9 %copy-done = bf16[1,2,128,256]{3,2,1,0:T(8,128)(2,1)S(1)} copy-done((bf16[1,2,128,256]{3,2,1,0:T(8,128)(2,1)S(1)}, bf16[1,2,128,256]{3,2,1,0:T(8,128)(2,1)}, u32[]{:S(2)}) %copy-start) | copy-done | bytes 131096
  0.9 0.9 %copy-done.1 = bf16[96,2,256]{2,1,0:T(2,128)(2,1)S(1)} copy-done((bf16[96,2,256]{2,1,0:T(2,128)(2,1)S(1)}, bf16[96,2,256]{2,1,0:T(2,128)(2,1)}, u32[]{:S(2)}) %copy-start.1) | copy-done | bytes 98328
  1.8 0.1 shard_map.37
  1.9 2.5 %collective-permute-start = (bf16[304,256]{1,0:T(8,128)(2,1)S(1)}, bf16[304,256]{1,0:T(8,128)(2,1)S(1)}, u32[]{:S(2)}, u32[]{:S(2)}) collective-permute-start(bf16[304,256]{1,0:T(8,128)(2,1)S(1)} %get-tuple-element.10), channel_id=1, source_target_pairs={{0,2},{2,4},{4,6},{6,0},{1,3},{3,5},{5,7},{7,1},{8,10},{10,12},{12... | collective-permute-start | bytes 466952 | tf_op jit(solution)/shard_map/ppermute | solution.py:182
  4.4 2.8 %collective-permute-start.1 = (bf16[304,256]{1,0:T(8,128)(2,1)S(1)}, bf16[304,256]{1,0:T(8,128)(2,1)S(1)}, u32[]{:S(2)}, u32[]{:S(2)}) collective-permute-start(bf16[304,256]{1,0:T(8,128)(2,1)S(1)} %get-tuple-element.11), channel_id=1, source_target_pairs={{0,6},{2,0},{4,2},{6,4},{1,7},{3,1},{5,3},{7,5},{8,14},{10,8},{12,... | collective-permute-start | bytes 466952 | tf_op jit(solution)/shard_map/ppermute | solution.py:182
  7.2 0.2 collective-permute-start.2
  7.4 3.6 %collective-permute-start.4 = (bf16[256,256]{1,0:T(8,128)(2,1)S(1)}, bf16[256,256]{1,0:T(8,128)(2,1)S(1)}, u32[]{:S(2)}, u32[]{:S(2)}) collective-permute-start(bf16[256,256]{1,0:T(8,128)(2,1)S(1)} %bitcast.15), channel_id=1, source_target_pairs={{0,134},{2,132},{4,130},{6,128},{128,6},{130,4},{132,2},{134,0},{1... | collective-permute-start | bytes 393224 | tf_op jit(solution)/shard_map/ppermute | solution.py:179
  11.7 1.8 %collective-permute-done.4.swapped_ref = bf16[256,256]{1,0:T(8,128)(2,1)S(1)} collective-permute-done((bf16[256,256]{1,0:T(8,128)(2,1)S(1)}, bf16[256,256]{1,0:T(8,128)(2,1)S(1)}, u32[]{:S(2)}, u32[]{:S(2)}) %collective-permute-start.4) | collective-permute-done | bytes 131104 | tf_op jit(solution)/shard_map/ppermute | solution.py:179
  13.5 0.7 %shard_map.38 = bf16[16,40,256]{2,1,0:T(8,128)(2,1)} custom-call(s32[1]{0:T(128)S(6)} %copy.5.kq_ref, bf16[256,256]{1,0:T(8,128)(2,1)S(1)} %bitcast.16, bf16[256,256]{1,0:T(8,128)(2,1)S(1)} %collective-permute-done.4.swapped_ref), custom_call_target="tpu_custom_call" | custom-call | tf_op jit(solution)/shard_map/pallas_call | solution.py:56
  14.2 6.6 %all-to-all-start = ((bf16[16,40,256]{2,1,0:T(8,128)(2,1)}), bf16[16,40,256]{2,1,0:T(8,128)(2,1)S(1)}, u32[]{:S(2)}, u32[]{:S(2)}) async-start(bf16[16,40,256]{2,1,0:T(8,128)(2,1)} %shard_map.38), calls=%async_computation | async-start | bytes 655360 | tf_op jit(solution)/shard_map/all_to_all | solution.py:181
  20.9 0.0 collective-permute-done
  20.9 0.8 %collective-permute-done.2 = bf16[304,256]{1,0:T(8,128)(2,1)S(1)} collective-permute-done((bf16[304,256]{1,0:T(8,128)(2,1)S(1)}, bf16[304,256]{1,0:T(8,128)(2,1)S(1)}, u32[]{:S(2)}, u32[]{:S(2)}) %collective-permute-start.2) | collective-permute-done | bytes 155680 | tf_op jit(solution)/shard_map/ppermute | solution.py:182
  21.7 0.1 pad_maximum_fusion.lines_ref
  21.8 2.1 %collective-permute-start.3 = (bf16[4,304,256]{2,1,0:T(8,128)(2,1)S(1)}, bf16[4,304,256]{2,1,0:T(8,128)(2,1)S(1)}, u32[]{:S(2)}, u32[]{:S(2)}) collective-permute-start(bf16[4,304,256]{2,1,0:T(8,128)(2,1)S(1)} %pad_maximum_fusion.lines_ref), channel_id=1, source_target_pairs={{0,1},{1,0},{2,3},{3,2},{4,5},{5,4},{6,7},{7,6},{8,9},{9,8},{10,11... | collective-permute-start | bytes 1867784 | tf_op jit(solution)/shard_map/ppermute | solution.py:184
  23.9 4.7 %all-to-all-done.ref = bf16[16,40,256]{2,1,0:T(8,128)(2,1)S(1)} async-done(((bf16[16,40,256]{2,1,0:T(8,128)(2,1)}), bf16[16,40,256]{2,1,0:T(8,128)(2,1)S(1)}, u32[]{:S(2)}, u32[]{:S(2)}) %all-to-all-start) | async-done | bytes 327712 | tf_op jit(solution)/shard_map/all_to_all | solution.py:181
  28.6 0.3 shard_map.39
  28.8 10.2 %all_to_all.10 = bf16[16,16,256]{2,1,0:T(8,128)(2,1)S(1)} all-to-all(bf16[16,16,256]{2,1,0:T(8,128)(2,1)S(1)} %shard_map.39), channel_id=1, replica_groups=mesh['zh'=2,'x'=4,'y'=4,'zl'=4,'c'=2] {'x','y'}, dimensions={0} | all-to-all | bytes 262144 | tf_op jit(solution)/shard_map/all_to_all | solution.py:185
  39.0 2.6 %collective-permute-start.8 = (bf16[256,256]{1,0:T(8,128)(2,1)S(1)}, bf16[256,256]{1,0:T(8,128)(2,1)S(1)}, u32[]{:S(2)}, u32[]{:S(2)}) collective-permute-start(bf16[256,256]{1,0:T(8,128)(2,1)S(1)} %bitcast.9), channel_id=1, source_target_pairs={{0,6},{2,0},{4,2},{6,4},{1,7},{3,1},{5,3},{7,5},{8,14},{10,8},{12,... | collective-permute-start | bytes 393224 | tf_op jit(solution)/shard_map/ppermute | solution.py:187
  41.6 9.2 %collective-permute-start.7 = (bf16[256,256]{1,0:T(8,128)(2,1)S(1)}, bf16[256,256]{1,0:T(8,128)(2,1)S(1)}, u32[]{:S(2)}, u32[]{:S(2)}) collective-permute-start(bf16[256,256]{1,0:T(8,128)(2,1)S(1)} %bitcast.10), channel_id=1, source_target_pairs={{0,2},{2,4},{4,6},{6,0},{1,3},{3,5},{5,7},{7,1},{8,10},{10,12},{12... | collective-permute-start | bytes 393224 | tf_op jit(solution)/shard_map/ppermute | solution.py:187
  50.7 1.2 %collective-permute-start.5 = (bf16[256,256]{1,0:T(8,128)(2,1)S(1)}, bf16[256,256]{1,0:T(8,128)(2,1)S(1)}, u32[]{:S(2)}, u32[]{:S(2)}) collective-permute-start(bf16[256,256]{1,0:T(8,128)(2,1)S(1)} %bitcast.11), channel_id=1, source_target_pairs={{0,4},{2,6},{4,0},{6,2},{1,5},{3,7},{5,1},{7,3},{8,12},{10,14},{12... | collective-permute-start | bytes 393224 | tf_op jit(solution)/shard_map/ppermute | solution.py:187
  51.9 4.8 %collective-permute-start.11 = (bf16[256,256]{1,0:T(8,128)(2,1)S(1)}, bf16[256,256]{1,0:T(8,128)(2,1)S(1)}, u32[]{:S(2)}, u32[]{:S(2)}) collective-permute-start(bf16[256,256]{1,0:T(8,128)(2,1)S(1)} %bitcast.12), channel_id=1, source_target_pairs={{0,1},{1,0},{2,3},{3,2},{4,5},{5,4},{6,7},{7,6},{8,9},{9,8},{10,11... | collective-permute-start | bytes 393224 | tf_op jit(solution)/shard_map/ppermute | solution.py:188
  56.7 0.7 %collective-permute-start.10 = (bf16[256,256]{1,0:T(8,128)(2,1)S(1)}, bf16[256,256]{1,0:T(8,128)(2,1)S(1)}, u32[]{:S(2)}, u32[]{:S(2)}) collective-permute-start(bf16[256,256]{1,0:T(8,128)(2,1)S(1)} %collective-permute-done.8.refs_1_), channel_id=1, source_target_pairs={{0,1},{1,0},{2,3},{3,2},{4,5},{5,4},{6,7},{7,6},{8,9},{9,8},{10,11... | collective-permute-start | bytes 393224 | tf_op jit(solution)/shard_map/ppermute | solution.py:188
  57.4 0.0 collective-permute-done.7.refs_0_
  57.4 3.2 %collective-permute-start.9 = (bf16[256,256]{1,0:T(8,128)(2,1)S(1)}, bf16[256,256]{1,0:T(8,128)(2,1)S(1)}, u32[]{:S(2)}, u32[]{:S(2)}) collective-permute-start(bf16[256,256]{1,0:T(8,128)(2,1)S(1)} %collective-permute-done.7.refs_0_), channel_id=1, source_target_pairs={{0,1},{1,0},{2,3},{3,2},{4,5},{5,4},{6,7},{7,6},{8,9},{9,8},{10,11... | collective-permute-start | bytes 393224 | tf_op jit(solution)/shard_map/ppermute | solution.py:188
  60.6 2.8 %collective-permute-done.5.refs_0_ = bf16[256,256]{1,0:T(8,128)(2,1)S(1)} collective-permute-done((bf16[256,256]{1,0:T(8,128)(2,1)S(1)}, bf16[256,256]{1,0:T(8,128)(2,1)S(1)}, u32[]{:S(2)}, u32[]{:S(2)}) %collective-permute-start.5) | collective-permute-done | bytes 131104 | tf_op jit(solution)/shard_map/ppermute | solution.py:187
  63.3 1.4 %collective-permute-start.6 = (bf16[256,256]{1,0:T(8,128)(2,1)S(1)}, bf16[256,256]{1,0:T(8,128)(2,1)S(1)}, u32[]{:S(2)}, u32[]{:S(2)}) collective-permute-start(bf16[256,256]{1,0:T(8,128)(2,1)S(1)} %collective-permute-done.5.refs_0_), channel_id=1, source_target_pairs={{0,1},{1,0},{2,3},{3,2},{4,5},{5,4},{6,7},{7,6},{8,9},{9,8},{10,11... | collective-permute-start | bytes 393224 | tf_op jit(solution)/shard_map/ppermute | solution.py:188
  64.8 0.0 collective-permute-done.11.refs_1_
  64.8 0.0 collective-permute-done.3.twins_ref
  64.8 1.1 %shard_map.40.refs_4_ = f32[12,2,128,128]{3,2,1,0:T(8,128)S(1)} custom-call(s32[1]{0:T(128)S(6)} %copy.5.kq_ref, bf16[4,304,256]{2,1,0:T(8,128)(2,1)S(1)} %pad_maximum_fusion.lines_ref, bf16[4,304,256]{2,1,0:T(8,128)(2,1)S(1)} %collective-permute-done.3.twins_ref, bf16[256,256]{1,0:T(8,128)(2,1)S(1)} %bitcast.13, ...), custom_call_target="tpu_custom_call" | custom-call | tf_op jit(solution)/shard_map/pallas_call | solution.py:164
  65.9 0.0 collective-permute-done.10.refs_3_
  65.9 2.0 %shard_map.41.refs_2_ = f32[12,2,128,128]{3,2,1,0:T(8,128)S(1)} custom-call(s32[1]{0:T(128)S(6)} %copy.5.kq_ref, bf16[4,304,256]{2,1,0:T(8,128)(2,1)S(1)} %pad_maximum_fusion.lines_ref, bf16[4,304,256]{2,1,0:T(8,128)(2,1)S(1)} %collective-permute-done.3.twins_ref, bf16[256,256]{1,0:T(8,128)(2,1)S(1)} %collective-permute-done.7.refs_0_, ...), custom_call_target="tpu_custom_call" | custom-call | tf_op jit(solution)/shard_map/pallas_call | solution.py:164
  67.9 1.9 %shard_map.42 = f32[12,2,128,128]{3,2,1,0:T(8,128)} custom-call(s32[1]{0:T(128)S(6)} %copy.5.kq_ref, bf16[4,304,256]{2,1,0:T(8,128)(2,1)S(1)} %pad_maximum_fusion.lines_ref, bf16[4,304,256]{2,1,0:T(8,128)(2,1)S(1)} %collective-permute-done.3.twins_ref, bf16[256,256]{1,0:T(8,128)(2,1)S(1)} %collective-permute-done.5.refs_0_, ...), custom_call_target="tpu_custom_call" | custom-call | tf_op jit(solution)/shard_map/pallas_call | solution.py:164
  (6 shorter events, 0.0 us)
Async XLA Ops:
  0.0 0.9 %copy-start = (bf16[1,2,128,256]{3,2,1,0:T(8,128)(2,1)S(1)}, bf16[1,2,128,256]{3,2,1,0:T(8,128)(2,1)}, u32[]{:S(2)}) copy-start(bf16[1,2,128,256]{3,2,1,0:T(8,128)(2,1)} %param.3) | copy-start | bytes 393220
  0.9 0.9 %copy-start.1 = (bf16[96,2,256]{2,1,0:T(2,128)(2,1)S(1)}, bf16[96,2,256]{2,1,0:T(2,128)(2,1)}, u32[]{:S(2)}) copy-start(bf16[96,2,256]{2,1,0:T(2,128)(2,1)} %pot_ref.1) | copy-start | bytes 294916
  1.9 19.0 %collective-permute-start = (bf16[304,256]{1,0:T(8,128)(2,1)S(1)}, bf16[304,256]{1,0:T(8,128)(2,1)S(1)}, u32[]{:S(2)}, u32[]{:S(2)}) collective-permute-start(bf16[304,256]{1,0:T(8,128)(2,1)S(1)} %get-tuple-element.10), channel_id=1, source_target_pairs={{0,2},{2,4},{4,6},{6,0},{1,3},{3,5},{5,7},{7,1},{8,10},{10,12},{12... | collective-permute-start | bytes 466952 | tf_op jit(solution)/shard_map/ppermute | solution.py:182
  4.4 16.5 %collective-permute-start.1 = (bf16[304,256]{1,0:T(8,128)(2,1)S(1)}, bf16[304,256]{1,0:T(8,128)(2,1)S(1)}, u32[]{:S(2)}, u32[]{:S(2)}) collective-permute-start(bf16[304,256]{1,0:T(8,128)(2,1)S(1)} %get-tuple-element.11), channel_id=1, source_target_pairs={{0,6},{2,0},{4,2},{6,4},{1,7},{3,1},{5,3},{7,5},{8,14},{10,8},{12,... | collective-permute-start | bytes 466952 | tf_op jit(solution)/shard_map/ppermute | solution.py:182
  7.2 14.4 %collective-permute-start.2 = (bf16[304,256]{1,0:T(8,128)(2,1)S(1)}, bf16[304,256]{1,0:T(8,128)(2,1)S(1)}, u32[]{:S(2)}, u32[]{:S(2)}) collective-permute-start(bf16[304,256]{1,0:T(8,128)(2,1)S(1)} %get-tuple-element.12), channel_id=1, source_target_pairs={{0,4},{2,6},{4,0},{6,2},{1,5},{3,7},{5,1},{7,3},{8,12},{10,14},{12... | collective-permute-start | bytes 466952 | tf_op jit(solution)/shard_map/ppermute | solution.py:182
  7.4 6.1 %collective-permute-start.4 = (bf16[256,256]{1,0:T(8,128)(2,1)S(1)}, bf16[256,256]{1,0:T(8,128)(2,1)S(1)}, u32[]{:S(2)}, u32[]{:S(2)}) collective-permute-start(bf16[256,256]{1,0:T(8,128)(2,1)S(1)} %bitcast.15), channel_id=1, source_target_pairs={{0,134},{2,132},{4,130},{6,128},{128,6},{130,4},{132,2},{134,0},{1... | collective-permute-start | bytes 393224 | tf_op jit(solution)/shard_map/ppermute | solution.py:179
  14.2 14.3 %all-to-all-start = ((bf16[16,40,256]{2,1,0:T(8,128)(2,1)}), bf16[16,40,256]{2,1,0:T(8,128)(2,1)S(1)}, u32[]{:S(2)}, u32[]{:S(2)}) async-start(bf16[16,40,256]{2,1,0:T(8,128)(2,1)} %shard_map.38), calls=%async_computation | async-start | bytes 655360 | tf_op jit(solution)/shard_map/all_to_all | solution.py:181
  21.8 43.0 %collective-permute-start.3 = (bf16[4,304,256]{2,1,0:T(8,128)(2,1)S(1)}, bf16[4,304,256]{2,1,0:T(8,128)(2,1)S(1)}, u32[]{:S(2)}, u32[]{:S(2)}) collective-permute-start(bf16[4,304,256]{2,1,0:T(8,128)(2,1)S(1)} %pad_maximum_fusion.lines_ref), channel_id=1, source_target_pairs={{0,1},{1,0},{2,3},{3,2},{4,5},{5,4},{6,7},{7,6},{8,9},{9,8},{10,11... | collective-permute-start | bytes 1867784 | tf_op jit(solution)/shard_map/ppermute | solution.py:184
  39.0 17.7 %collective-permute-start.8 = (bf16[256,256]{1,0:T(8,128)(2,1)S(1)}, bf16[256,256]{1,0:T(8,128)(2,1)S(1)}, u32[]{:S(2)}, u32[]{:S(2)}) collective-permute-start(bf16[256,256]{1,0:T(8,128)(2,1)S(1)} %bitcast.9), channel_id=1, source_target_pairs={{0,6},{2,0},{4,2},{6,4},{1,7},{3,1},{5,3},{7,5},{8,14},{10,8},{12,... | collective-permute-start | bytes 393224 | tf_op jit(solution)/shard_map/ppermute | solution.py:187
  41.6 15.8 %collective-permute-start.7 = (bf16[256,256]{1,0:T(8,128)(2,1)S(1)}, bf16[256,256]{1,0:T(8,128)(2,1)S(1)}, u32[]{:S(2)}, u32[]{:S(2)}) collective-permute-start(bf16[256,256]{1,0:T(8,128)(2,1)S(1)} %bitcast.10), channel_id=1, source_target_pairs={{0,2},{2,4},{4,6},{6,0},{1,3},{3,5},{5,7},{7,1},{8,10},{10,12},{12... | collective-permute-start | bytes 393224 | tf_op jit(solution)/shard_map/ppermute | solution.py:187
  50.7 12.6 %collective-permute-start.5 = (bf16[256,256]{1,0:T(8,128)(2,1)S(1)}, bf16[256,256]{1,0:T(8,128)(2,1)S(1)}, u32[]{:S(2)}, u32[]{:S(2)}) collective-permute-start(bf16[256,256]{1,0:T(8,128)(2,1)S(1)} %bitcast.11), channel_id=1, source_target_pairs={{0,4},{2,6},{4,0},{6,2},{1,5},{3,7},{5,1},{7,3},{8,12},{10,14},{12... | collective-permute-start | bytes 393224 | tf_op jit(solution)/shard_map/ppermute | solution.py:187
  51.9 12.9 %collective-permute-start.11 = (bf16[256,256]{1,0:T(8,128)(2,1)S(1)}, bf16[256,256]{1,0:T(8,128)(2,1)S(1)}, u32[]{:S(2)}, u32[]{:S(2)}) collective-permute-start(bf16[256,256]{1,0:T(8,128)(2,1)S(1)} %bitcast.12), channel_id=1, source_target_pairs={{0,1},{1,0},{2,3},{3,2},{4,5},{5,4},{6,7},{7,6},{8,9},{9,8},{10,11... | collective-permute-start | bytes 393224 | tf_op jit(solution)/shard_map/ppermute | solution.py:188
  56.7 9.2 %collective-permute-start.10 = (bf16[256,256]{1,0:T(8,128)(2,1)S(1)}, bf16[256,256]{1,0:T(8,128)(2,1)S(1)}, u32[]{:S(2)}, u32[]{:S(2)}) collective-permute-start(bf16[256,256]{1,0:T(8,128)(2,1)S(1)} %collective-permute-done.8.refs_1_), channel_id=1, source_target_pairs={{0,1},{1,0},{2,3},{3,2},{4,5},{5,4},{6,7},{7,6},{8,9},{9,8},{10,11... | collective-permute-start | bytes 393224 | tf_op jit(solution)/shard_map/ppermute | solution.py:188
  57.4 8.5 %collective-permute-start.9 = (bf16[256,256]{1,0:T(8,128)(2,1)S(1)}, bf16[256,256]{1,0:T(8,128)(2,1)S(1)}, u32[]{:S(2)}, u32[]{:S(2)}) collective-permute-start(bf16[256,256]{1,0:T(8,128)(2,1)S(1)} %collective-permute-done.7.refs_0_), channel_id=1, source_target_pairs={{0,1},{1,0},{2,3},{3,2},{4,5},{5,4},{6,7},{7,6},{8,9},{9,8},{10,11... | collective-permute-start | bytes 393224 | tf_op jit(solution)/shard_map/ppermute | solution.py:188
  63.3 4.6 %collective-permute-start.6 = (bf16[256,256]{1,0:T(8,128)(2,1)S(1)}, bf16[256,256]{1,0:T(8,128)(2,1)S(1)}, u32[]{:S(2)}, u32[]{:S(2)}) collective-permute-start(bf16[256,256]{1,0:T(8,128)(2,1)S(1)} %collective-permute-done.5.refs_0_), channel_id=1, source_target_pairs={{0,1},{1,0},{2,3},{3,2},{4,5},{5,4},{6,7},{7,6},{8,9},{9,8},{10,11... | collective-permute-start | bytes 393224 | tf_op jit(solution)/shard_map/ppermute | solution.py:188

commit v3 on v2

--- a/solution.py
+++ b/solution.py
@@ -8,11 +8,9 @@
 
 KA = ("zh", "x", "y")
 GA = ("zl", "c")
-XY = ("x", "y")
 SWAP = [(0, 1), (1, 0)]
 MIRROR = [(z, 7 - z) for z in range(8)]
 STEPS = (0, 1, 3, 2)
-TAG = 8
 SMALL = pltpu.CompilerParams(vmem_limit_bytes=20 * 2**20)
 IN_SMEM = pl.BlockSpec(memory_space=pltpu.SMEM)
 IN_VMEM = pl.BlockSpec(memory_space=pltpu.VMEM)
@@ -42,42 +40,59 @@
     )(slab, potential)
 
 
-def pack_spread(slab, swapped, kq):
-    rows, cells = slab.shape
-    piece = rows // 16
-
-    def kernel(kq_ref, slab_ref, swapped_ref, out):
-        tag = jnp.full((TAG, cells), kq_ref[0].astype(jnp.float32)).astype(slab.dtype)
-        for j in range(16):
-            out[j, :piece] = slab_ref[j * piece : (j + 1) * piece]
-            out[j, piece : 2 * piece] = swapped_ref[j * piece : (j + 1) * piece]
-            out[j, 2 * piece :] = tag
-
-    return pl.pallas_call(
-        kernel,
-        in_specs=[IN_SMEM, IN_VMEM, IN_VMEM],
-        out_shape=jax.ShapeDtypeStruct((16, 2 * piece + TAG, cells), slab.dtype),
-        compiler_params=SMALL,
-    )(kq, slab, swapped)
-
-
-def choose(pieces):
-    count, rows, cells = pieces.shape
-    piece = (rows - TAG) // 2
-
-    def kernel(ref, out):
-        zh = lax.axis_index("zh")
-        for d in range(count):
-            source = jnp.max(ref[d, 2 * piece :, :128].astype(jnp.float32)).astype(jnp.int32)
-            side = jnp.where(source // count == zh, 0, piece)
-            out[d] = ref[lax.rem(source, count), pl.ds(pl.multiple_of(side, piece), piece), :]
-
-    return pl.pallas_call(
-        kernel,
-        in_specs=[IN_VMEM],
-        out_shape=jax.ShapeDtypeStruct((count, piece, cells), pieces.dtype),
-        compiler_params=SMALL,
-    )(pieces)
+def number_in(ref):
+    return jnp.max(ref[...].astype(jnp.float32)).astype(jnp.int32)
+
+
+def pick(number, values):
+    out = values[0]
+    for i, value in enumerate(values[1:], 1):
+        out = jnp.where(number == i, value, out)
+    return out
+
+
+def choose(wanted, blocks):
+    count = len(wanted)
+    rows, cells = blocks[0].shape
+
+    def kernel(*refs):
+        numbers = [number_in(ref) for ref in refs[:count]]
+        held, outs = refs[count : count + len(blocks)], refs[count + len(blocks) :]
+        zh, y = lax.axis_index("zh"), lax.axis_index("y")
+        places = []
+        for number in numbers:
+            back = lax.rem(y + 4 - lax.rem(number, 4), 4)
+            back = jnp.where(back == 2, 3, jnp.where(back == 3, 2, back))
+            places.append(jnp.where(number // 16 == zh, back, back + 4))
+        for at in range(0, rows, 16):
+            values = [ref[at : at + 16] for ref in held]
+            for place, out in zip(places, outs):
+                out[at : at + 16] = pick(place, values)
+
+    return pl.pallas_call(
+        kernel,
+        in_specs=[IN_VMEM] * (count + len(blocks)),
+        out_shape=[jax.ShapeDtypeStruct((rows, cells), blocks[0].dtype)] * count,
+        compiler_params=SMALL,
+    )(*wanted, *blocks)
+
+
+def keep(own, came):
+    rows, cells = came[0].shape
+
+    def kernel(own_ref, *refs):
+        number = number_in(own_ref)
+        back = lax.rem(lax.axis_index("x") + 4 - lax.rem(number // 4, 4), 4)
+        back = jnp.where(back == 2, 3, jnp.where(back == 3, 2, back))
+        for at in range(0, rows, 16):
+            refs[-1][at : at + 16] = pick(back, [ref[at : at + 16] for ref in refs[:-1]])
+
+    return pl.pallas_call(
+        kernel,
+        in_specs=[IN_VMEM] * (1 + len(came)),
+        out_shape=jax.ShapeDtypeStruct((rows, cells), came[0].dtype),
+        compiler_params=SMALL,
+    )(own, *came)
 
 
 def couple(kq, lines, twins, others, steps, bands, modes, last, before=None):
@@ -178,11 +193,16 @@
 
     swapped = lax.ppermute(slab, ("zh", "zl"), MIRROR)
     packs = pack_lines(slab, dvscf)
-    pieces = lax.all_to_all(pack_spread(slab, swapped, kq_map), XY, 0, 0, tiled=True)
+    tag = jnp.broadcast_to(kq_map, (8, 128))
+    near = [slab] + [lax.ppermute(slab, "y", ring(STEPS[i])) for i in (1, 2, 3)]
+    far = [swapped] + [lax.ppermute(swapped, "y", ring(STEPS[i])) for i in (1, 2, 3)]
+    wanted = [tag] + [lax.ppermute(tag, "x", ring(-STEPS[i])) for i in (1, 2, 3)]
     lines = [packs[0]] + [lax.ppermute(packs[i], "zl", ring(STEPS[i])) for i in (1, 2, 3)]
     lines = jnp.stack(lines)
     twins = lax.ppermute(lines, "c", SWAP)
-    phi = lax.all_to_all(choose(pieces), XY, 0, 0, tiled=True).reshape(2 * bands, cells)
+    slots = choose(wanted, near + far)
+    came = [slots[0]] + [lax.ppermute(slots[i], "x", ring(STEPS[i])) for i in (1, 2, 3)]
+    phi = keep(tag, came)
 
     others = [phi] + [lax.ppermute(phi, "zl", ring(STEPS[i])) for i in (1, 2, 3)]
     mates = [lax.ppermute(o, "c", SWAP) for o in others]

time: 70.2 us -> 77.3 us (1.10)
  waiting for transfers between devices: 10.1 us -> 27 us
  blocking collectives: 10.2 us -> 0 us
  starting transfers between devices: 40.8 us -> 41.7 us
    ppermute x0 -> x12, waiting for transfers between devices: none -> 19.1 us  [the longest x3 7.25 us: body(): lax.ppermute(tag, 'x', ring(-STEPS[i]))]
    ppermute x0 -> x12, starting transfers between devices: none -> 15 us  [the longest x3 5.66 us: body(): near = [slab] + [lax.ppermute(slab, 'y', ring(STEPS[i])) for i in (1, 2, 3)]]
    all_to_all x1 -> x0, blocking collectives: 10.2 us -> none  [body(): lax.all_to_all(choose(pieces), XY, 0, 0, tiled=True)]
    ppermute x3, starting transfers between devices: 12.9 us -> 3.52 us  [body(): lax.ppermute(phi, 'zl', ring(STEPS[i]))]
    ppermute x3, waiting for transfers between devices: 0.78 us -> 7.92 us  [body(): lax.ppermute(packs[i], 'zl', ring(STEPS[i]))]
    all_to_all x1 -> x0, starting transfers between devices: 6.64 us -> none  [body(): lax.all_to_all(pack_spread(slab, swapped, kq_map), XY, 0, 0, tiled=True)]
    all_to_all x1 -> x0, waiting for transfers between devices: 4.72 us -> none  [body(): lax.all_to_all(pack_spread(slab, swapped, kq_map), XY, 0, 0, tiled=True)]
    ppermute x4, starting transfers between devices: 10.1 us -> 13.4 us  [body(): mates = [lax.ppermute(o, 'c', SWAP) for o in others]]
  transfers between devices with their start and end apart: 13 -> 24, of which waited for: 4 -> 10; matrix products, arithmetic and copies ran while one was open for 0% -> 0% of each run, Pallas kernels for 6% -> 5%
where the time goes in v3:
time: 77.3 us; the launch traced here: 77.2 us
  starting transfers between devices  41.7 us (54%)
  waiting for transfers between devices  27 us (35%)
  Pallas kernels  5.62 us (7%)
  local copies, waits for them, and re-layouts  1.8 us (2%)
  between operations  0.92 us (1%)
    ppermute x4, starting transfers between devices, body(): mates = [lax.ppermute(o, 'c', SWAP) for o in others]  13.4 us
    ppermute x3, waiting for transfers between devices, body(): lax.ppermute(packs[i], 'zl', ring(STEPS[i]))  7.92 us
    ppermute x3, waiting for transfers between devices, body(): lax.ppermute(tag, 'x', ring(-STEPS[i]))  7.25 us
    ppermute x3, waiting for transfers between devices, body(): lax.ppermute(swapped, 'y', ring(STEPS[i]))  6.5 us
    ppermute x3, starting transfers between devices, body(): near = [slab] + [lax.ppermute(slab, 'y', ring(STEPS[i])) for i in (1, 2, 3)]  5.66 us
    ppermute x3, starting transfers between devices, body(): lax.ppermute(packs[i], 'zl', ring(STEPS[i]))  5.53 us
    ppermute x3, waiting for transfers between devices, body(): lax.ppermute(slots[i], 'x', ring(STEPS[i]))  5.32 us
    pallas_call x3, Pallas kernels, couple(): pl.pallas_call(kernel, in_specs=specs, out_specs=pl.BlockSpec(memory_spac...  5.02 us
  transfers between devices with their start and end apart: 24, of which 10 were waited for; matrix products, arithmetic and copies ran while one was open for 0% of the time, Pallas kernels for 5%

profile of v3, /device:TPU:1, one launch (start us, length us, event | category | flops | bytes accessed | tf_op | source)
XLA Modules:
  0.0 77.2 jit_solution(9767615107158498238)
XLA Ops:
  0.0 0.9 %copy-done = bf16[1,2,128,256]{3,2,1,0:T(8,128)(2,1)S(1)} copy-done((bf16[1,2,128,256]{3,2,1,0:T(8,128)(2,1)S(1)}, bf16[1,2,128,256]{3,2,1,0:T(8,128)(2,1)}, u32[]{:S(2)}) %copy-start) | copy-done | bytes 131096
  0.9 0.9 %copy-done.1 = bf16[96,2,256]{2,1,0:T(2,128)(2,1)S(1)} copy-done((bf16[96,2,256]{2,1,0:T(2,128)(2,1)S(1)}, bf16[96,2,256]{2,1,0:T(2,128)(2,1)}, u32[]{:S(2)}) %copy-start.1) | copy-done | bytes 98328
  1.9 2.5 %collective-permute-start = (bf16[304,256]{1,0:T(8,128)(2,1)S(1)}, bf16[304,256]{1,0:T(8,128)(2,1)S(1)}, u32[]{:S(2)}, u32[]{:S(2)}) collective-permute-start(bf16[304,256]{1,0:T(8,128)(2,1)S(1)} %get-tuple-element.14), channel_id=1, source_target_pairs={{0,2},{2,4},{4,6},{6,0},{1,3},{3,5},{5,7},{7,1},{8,10},{10,12},{12... | collective-permute-start | bytes 466952 | tf_op jit(solution)/shard_map/ppermute | solution.py:200
  4.4 2.8 %collective-permute-start.1 = (bf16[304,256]{1,0:T(8,128)(2,1)S(1)}, bf16[304,256]{1,0:T(8,128)(2,1)S(1)}, u32[]{:S(2)}, u32[]{:S(2)}) collective-permute-start(bf16[304,256]{1,0:T(8,128)(2,1)S(1)} %get-tuple-element.15), channel_id=1, source_target_pairs={{0,6},{2,0},{4,2},{6,4},{1,7},{3,1},{5,3},{7,5},{8,14},{10,8},{12,... | collective-permute-start | bytes 466952 | tf_op jit(solution)/shard_map/ppermute | solution.py:200
  7.4 3.6 %collective-permute-start.10 = (bf16[256,256]{1,0:T(8,128)(2,1)S(1)}, bf16[256,256]{1,0:T(8,128)(2,1)S(1)}, u32[]{:S(2)}, u32[]{:S(2)}) collective-permute-start(bf16[256,256]{1,0:T(8,128)(2,1)S(1)} %bitcast.11), channel_id=1, source_target_pairs={{0,134},{2,132},{4,130},{6,128},{128,6},{130,4},{132,2},{134,0},{1... | collective-permute-start | bytes 393224 | tf_op jit(solution)/shard_map/ppermute | solution.py:194
  11.0 1.3 %collective-permute-start.7 = (bf16[256,256]{1,0:T(8,128)(2,1)S(1)}, bf16[256,256]{1,0:T(8,128)(2,1)S(1)}, u32[]{:S(2)}, u32[]{:S(2)}) collective-permute-start(bf16[256,256]{1,0:T(8,128)(2,1)S(1)} %bitcast.12), channel_id=1, source_target_pairs={{0,8},{8,16},{16,24},{24,0},{1,9},{9,17},{17,25},{25,1},{2,10},{10... | collective-permute-start | bytes 393224 | tf_op jit(solution)/shard_map/ppermute | solution.py:197
  12.3 1.4 %collective-permute-start.8 = (bf16[256,256]{1,0:T(8,128)(2,1)S(1)}, bf16[256,256]{1,0:T(8,128)(2,1)S(1)}, u32[]{:S(2)}, u32[]{:S(2)}) collective-permute-start(bf16[256,256]{1,0:T(8,128)(2,1)S(1)} %bitcast.13), channel_id=1, source_target_pairs={{0,24},{8,0},{16,8},{24,16},{1,25},{9,1},{17,9},{25,17},{2,26},{10... | collective-permute-start | bytes 393224 | tf_op jit(solution)/shard_map/ppermute | solution.py:197
  13.8 7.9 %collective-permute-done.2 = bf16[304,256]{1,0:T(8,128)(2,1)S(1)} collective-permute-done((bf16[304,256]{1,0:T(8,128)(2,1)S(1)}, bf16[304,256]{1,0:T(8,128)(2,1)S(1)}, u32[]{:S(2)}, u32[]{:S(2)}) %collective-permute-start.2) | collective-permute-done | bytes 155680 | tf_op jit(solution)/shard_map/ppermute | solution.py:200
  21.8 0.6 collective-permute-start.3
  23.1 2.6 %collective-permute-start.4 = (s32[8,128]{1,0:T(8,128)S(1)}, s32[8,128]{1,0:T(8,128)S(1)}, u32[]{:S(2)}, u32[]{:S(2)}) collective-permute-start(s32[8,128]{1,0:T(8,128)S(1)} %broadcast_in_dim.8.refs_0_.own_ref), channel_id=1, source_target_pairs={{0,96},{32,0},{64,32},{96,64},{1,97},{33,1},{65,33},{97,65},{2,98}... | collective-permute-start | bytes 12296 | tf_op jit(solution)/shard_map/ppermute | solution.py:199
  25.6 0.8 collective-permute-done.4.refs_1_
  26.4 0.4 collective-permute-start.5
  26.8 3.5 %collective-permute-done.5.refs_2_ = s32[8,128]{1,0:T(8,128)S(1)} collective-permute-done((s32[8,128]{1,0:T(8,128)S(1)}, s32[8,128]{1,0:T(8,128)S(1)}, u32[]{:S(2)}, u32[]{:S(2)}) %collective-permute-start.5) | collective-permute-done | bytes 4128 | tf_op jit(solution)/shard_map/ppermute | solution.py:199
  30.3 0.9 %collective-permute-start.6 = (s32[8,128]{1,0:T(8,128)S(1)}, s32[8,128]{1,0:T(8,128)S(1)}, u32[]{:S(2)}, u32[]{:S(2)}) collective-permute-start(s32[8,128]{1,0:T(8,128)S(1)} %broadcast_in_dim.8.refs_0_.own_ref), channel_id=1, source_target_pairs={{0,64},{32,96},{64,0},{96,32},{1,65},{33,97},{65,1},{97,33},{2,66}... | collective-permute-start | bytes 12296 | tf_op jit(solution)/shard_map/ppermute | solution.py:199
  31.2 3.0 %collective-permute-done.6.refs_3_ = s32[8,128]{1,0:T(8,128)S(1)} collective-permute-done((s32[8,128]{1,0:T(8,128)S(1)}, s32[8,128]{1,0:T(8,128)S(1)}, u32[]{:S(2)}, u32[]{:S(2)}) %collective-permute-start.6) | collective-permute-done | bytes 4128 | tf_op jit(solution)/shard_map/ppermute | solution.py:199
  34.3 2.9 %collective-permute-start.9 = (bf16[256,256]{1,0:T(8,128)(2,1)S(1)}, bf16[256,256]{1,0:T(8,128)(2,1)S(1)}, u32[]{:S(2)}, u32[]{:S(2)}) collective-permute-start(bf16[256,256]{1,0:T(8,128)(2,1)S(1)} %bitcast.14), channel_id=1, source_target_pairs={{0,16},{8,24},{16,0},{24,8},{1,17},{9,25},{17,1},{25,9},{2,18},{10... | collective-permute-start | bytes 393224 | tf_op jit(solution)/shard_map/ppermute | solution.py:197
  37.2 0.4 collective-permute-start.11
  37.6 2.3 %collective-permute-start.12 = (bf16[256,256]{1,0:T(8,128)(2,1)S(1)}, bf16[256,256]{1,0:T(8,128)(2,1)S(1)}, u32[]{:S(2)}, u32[]{:S(2)}) collective-permute-start(bf16[256,256]{1,0:T(8,128)(2,1)S(1)} %collective-permute-done.10.refs_8_), channel_id=1, source_target_pairs={{0,24},{8,0},{16,8},{24,16},{1,25},{9,1},{17,9},{25,17},{2,26},{10... | collective-permute-start | bytes 393224 | tf_op jit(solution)/shard_map/ppermute | solution.py:198
  39.9 3.7 %collective-permute-done.11.refs_9_ = bf16[256,256]{1,0:T(8,128)(2,1)S(1)} collective-permute-done((bf16[256,256]{1,0:T(8,128)(2,1)S(1)}, bf16[256,256]{1,0:T(8,128)(2,1)S(1)}, u32[]{:S(2)}, u32[]{:S(2)}) %collective-permute-start.11) | collective-permute-done | bytes 131104 | tf_op jit(solution)/shard_map/ppermute | solution.py:198
  43.6 1.0 %collective-permute-done.12.refs_10_ = bf16[256,256]{1,0:T(8,128)(2,1)S(1)} collective-permute-done((bf16[256,256]{1,0:T(8,128)(2,1)S(1)}, bf16[256,256]{1,0:T(8,128)(2,1)S(1)}, u32[]{:S(2)}, u32[]{:S(2)}) %collective-permute-start.12) | collective-permute-done | bytes 131104 | tf_op jit(solution)/shard_map/ppermute | solution.py:198
  44.6 1.8 %collective-permute-done.13.refs_11_ = bf16[256,256]{1,0:T(8,128)(2,1)S(1)} collective-permute-done((bf16[256,256]{1,0:T(8,128)(2,1)S(1)}, bf16[256,256]{1,0:T(8,128)(2,1)S(1)}, u32[]{:S(2)}, u32[]{:S(2)}) %collective-permute-start.13) | collective-permute-done | bytes 131104 | tf_op jit(solution)/shard_map/ppermute | solution.py:198
  46.8 2.7 %collective-permute-start.15 = (bf16[256,256]{1,0:T(8,128)(2,1)S(1)}, bf16[256,256]{1,0:T(8,128)(2,1)S(1)}, u32[]{:S(2)}, u32[]{:S(2)}) collective-permute-start(bf16[256,256]{1,0:T(8,128)(2,1)S(1)} %get-tuple-element.19), channel_id=1, source_target_pairs={{0,96},{32,0},{64,32},{96,64},{1,97},{33,1},{65,33},{97,65},{2,98}... | collective-permute-start | bytes 393224 | tf_op jit(solution)/shard_map/ppermute | solution.py:204
  49.5 2.3 %collective-permute-done.14.refs_1_ = bf16[256,256]{1,0:T(8,128)(2,1)S(1)} collective-permute-done((bf16[256,256]{1,0:T(8,128)(2,1)S(1)}, bf16[256,256]{1,0:T(8,128)(2,1)S(1)}, u32[]{:S(2)}, u32[]{:S(2)}) %collective-permute-start.14) | collective-permute-done | bytes 131104 | tf_op jit(solution)/shard_map/ppermute | solution.py:204
  51.8 1.0 %collective-permute-done.15.refs_2_ = bf16[256,256]{1,0:T(8,128)(2,1)S(1)} collective-permute-done((bf16[256,256]{1,0:T(8,128)(2,1)S(1)}, bf16[256,256]{1,0:T(8,128)(2,1)S(1)}, u32[]{:S(2)}, u32[]{:S(2)}) %collective-permute-start.15) | collective-permute-done | bytes 131104 | tf_op jit(solution)/shard_map/ppermute | solution.py:204
  52.8 2.0 %collective-permute-done.16.refs_3_ = bf16[256,256]{1,0:T(8,128)(2,1)S(1)} collective-permute-done((bf16[256,256]{1,0:T(8,128)(2,1)S(1)}, bf16[256,256]{1,0:T(8,128)(2,1)S(1)}, u32[]{:S(2)}, u32[]{:S(2)}) %collective-permute-start.16) | collective-permute-done | bytes 131104 | tf_op jit(solution)/shard_map/ppermute | solution.py:204
  55.2 3.3 %collective-permute-start.20 = (bf16[256,256]{1,0:T(8,128)(2,1)S(1)}, bf16[256,256]{1,0:T(8,128)(2,1)S(1)}, u32[]{:S(2)}, u32[]{:S(2)}) collective-permute-start(bf16[256,256]{1,0:T(8,128)(2,1)S(1)} %shard_map.42.refs_0_), channel_id=1, source_target_pairs={{0,6},{2,0},{4,2},{6,4},{1,7},{3,1},{5,3},{7,5},{8,14},{10,8},{12,... | collective-permute-start | bytes 393224 | tf_op jit(solution)/shard_map/ppermute | solution.py:207
  58.5 6.3 %collective-permute-start.23 = (bf16[256,256]{1,0:T(8,128)(2,1)S(1)}, bf16[256,256]{1,0:T(8,128)(2,1)S(1)}, u32[]{:S(2)}, u32[]{:S(2)}) collective-permute-start(bf16[256,256]{1,0:T(8,128)(2,1)S(1)} %shard_map.42.refs_0_), channel_id=1, source_target_pairs={{0,1},{1,0},{2,3},{3,2},{4,5},{5,4},{6,7},{7,6},{8,9},{9,8},{10,11... | collective-permute-start | bytes 393224 | tf_op jit(solution)/shard_map/ppermute | solution.py:208
  64.7 3.0 %collective-permute-start.21 = (bf16[256,256]{1,0:T(8,128)(2,1)S(1)}, bf16[256,256]{1,0:T(8,128)(2,1)S(1)}, u32[]{:S(2)}, u32[]{:S(2)}) collective-permute-start(bf16[256,256]{1,0:T(8,128)(2,1)S(1)} %collective-permute-done.19.refs_0_), channel_id=1, source_target_pairs={{0,1},{1,0},{2,3},{3,2},{4,5},{5,4},{6,7},{7,6},{8,9},{9,8},{10,11... | collective-permute-start | bytes 393224 | tf_op jit(solution)/shard_map/ppermute | solution.py:208
  68.2 3.8 %collective-permute-start.18 = (bf16[256,256]{1,0:T(8,128)(2,1)S(1)}, bf16[256,256]{1,0:T(8,128)(2,1)S(1)}, u32[]{:S(2)}, u32[]{:S(2)}) collective-permute-start(bf16[256,256]{1,0:T(8,128)(2,1)S(1)} %collective-permute-done.17.refs_0_), channel_id=1, source_target_pairs={{0,1},{1,0},{2,3},{3,2},{4,5},{5,4},{6,7},{7,6},{8,9},{9,8},{10,11... | collective-permute-start | bytes 393224 | tf_op jit(solution)/shard_map/ppermute | solution.py:208
  71.9 1.1 %shard_map.43.refs_4_ = f32[12,2,128,128]{3,2,1,0:T(8,128)S(1)} custom-call(s32[1]{0:T(128)} %copy.5.kq_ref, bf16[4,304,256]{2,1,0:T(8,128)(2,1)S(1)} %pad_maximum_fusion.lines_ref, bf16[4,304,256]{2,1,0:T(8,128)(2,1)S(1)} %collective-permute-done.3.twins_ref, bf16[256,256]{1,0:T(8,128)(2,1)S(1)} %shard_map.42.refs_0_, ...), custom_call_target="tpu_custom_call" | custom-call | tf_op jit(solution)/shard_map/pallas_call | solution.py:179
  73.1 2.0 %shard_map.44.refs_2_ = f32[12,2,128,128]{3,2,1,0:T(8,128)S(1)} custom-call(s32[1]{0:T(128)} %copy.5.kq_ref, bf16[4,304,256]{2,1,0:T(8,128)(2,1)S(1)} %pad_maximum_fusion.lines_ref, bf16[4,304,256]{2,1,0:T(8,128)(2,1)S(1)} %collective-permute-done.3.twins_ref, bf16[256,256]{1,0:T(8,128)(2,1)S(1)} %collective-permute-done.19.refs_0_, ...), custom_call_target="tpu_custom_call" | custom-call | tf_op jit(solution)/shard_map/pallas_call | solution.py:179
  75.1 1.9 %shard_map.45 = f32[12,2,128,128]{3,2,1,0:T(8,128)} custom-call(s32[1]{0:T(128)} %copy.5.kq_ref, bf16[4,304,256]{2,1,0:T(8,128)(2,1)S(1)} %pad_maximum_fusion.lines_ref, bf16[4,304,256]{2,1,0:T(8,128)(2,1)S(1)} %collective-permute-done.3.twins_ref, bf16[256,256]{1,0:T(8,128)(2,1)S(1)} %collective-permute-done.17.refs_0_, ...), custom_call_target="tpu_custom_call" | custom-call | tf_op jit(solution)/shard_map/pallas_call | solution.py:179
  (28 shorter events, 1.7 us)
Async XLA Ops:
  0.0 0.9 %copy-start = (bf16[1,2,128,256]{3,2,1,0:T(8,128)(2,1)S(1)}, bf16[1,2,128,256]{3,2,1,0:T(8,128)(2,1)}, u32[]{:S(2)}) copy-start(bf16[1,2,128,256]{3,2,1,0:T(8,128)(2,1)} %param.3) | copy-start | bytes 393220
  0.9 0.9 %copy-start.1 = (bf16[96,2,256]{2,1,0:T(2,128)(2,1)S(1)}, bf16[96,2,256]{2,1,0:T(2,128)(2,1)}, u32[]{:S(2)}) copy-start(bf16[96,2,256]{2,1,0:T(2,128)(2,1)} %pot_ref.1) | copy-start | bytes 294916
  1.9 10.4 %collective-permute-start = (bf16[304,256]{1,0:T(8,128)(2,1)S(1)}, bf16[304,256]{1,0:T(8,128)(2,1)S(1)}, u32[]{:S(2)}, u32[]{:S(2)}) collective-permute-start(bf16[304,256]{1,0:T(8,128)(2,1)S(1)} %get-tuple-element.14), channel_id=1, source_target_pairs={{0,2},{2,4},{4,6},{6,0},{1,3},{3,5},{5,7},{7,1},{8,10},{10,12},{12... | collective-permute-start | bytes 466952 | tf_op jit(solution)/shard_map/ppermute | solution.py:200
  4.4 9.3 %collective-permute-start.1 = (bf16[304,256]{1,0:T(8,128)(2,1)S(1)}, bf16[304,256]{1,0:T(8,128)(2,1)S(1)}, u32[]{:S(2)}, u32[]{:S(2)}) collective-permute-start(bf16[304,256]{1,0:T(8,128)(2,1)S(1)} %get-tuple-element.15), channel_id=1, source_target_pairs={{0,6},{2,0},{4,2},{6,4},{1,7},{3,1},{5,3},{7,5},{8,14},{10,8},{12,... | collective-permute-start | bytes 466952 | tf_op jit(solution)/shard_map/ppermute | solution.py:200
  7.2 14.4 %collective-permute-start.2 = (bf16[304,256]{1,0:T(8,128)(2,1)S(1)}, bf16[304,256]{1,0:T(8,128)(2,1)S(1)}, u32[]{:S(2)}, u32[]{:S(2)}) collective-permute-start(bf16[304,256]{1,0:T(8,128)(2,1)S(1)} %get-tuple-element.16), channel_id=1, source_target_pairs={{0,4},{2,6},{4,0},{6,2},{1,5},{3,7},{5,1},{7,3},{8,12},{10,14},{12... | collective-permute-start | bytes 466952 | tf_op jit(solution)/shard_map/ppermute | solution.py:200
  7.4 29.7 %collective-permute-start.10 = (bf16[256,256]{1,0:T(8,128)(2,1)S(1)}, bf16[256,256]{1,0:T(8,128)(2,1)S(1)}, u32[]{:S(2)}, u32[]{:S(2)}) collective-permute-start(bf16[256,256]{1,0:T(8,128)(2,1)S(1)} %bitcast.11), channel_id=1, source_target_pairs={{0,134},{2,132},{4,130},{6,128},{128,6},{130,4},{132,2},{134,0},{1... | collective-permute-start | bytes 393224 | tf_op jit(solution)/shard_map/ppermute | solution.py:194
  11.0 26.6 %collective-permute-start.7 = (bf16[256,256]{1,0:T(8,128)(2,1)S(1)}, bf16[256,256]{1,0:T(8,128)(2,1)S(1)}, u32[]{:S(2)}, u32[]{:S(2)}) collective-permute-start(bf16[256,256]{1,0:T(8,128)(2,1)S(1)} %bitcast.12), channel_id=1, source_target_pairs={{0,8},{8,16},{16,24},{24,0},{1,9},{9,17},{17,25},{25,1},{2,10},{10... | collective-permute-start | bytes 393224 | tf_op jit(solution)/shard_map/ppermute | solution.py:197
  12.3 27.5 %collective-permute-start.8 = (bf16[256,256]{1,0:T(8,128)(2,1)S(1)}, bf16[256,256]{1,0:T(8,128)(2,1)S(1)}, u32[]{:S(2)}, u32[]{:S(2)}) collective-permute-start(bf16[256,256]{1,0:T(8,128)(2,1)S(1)} %bitcast.13), channel_id=1, source_target_pairs={{0,24},{8,0},{16,8},{24,16},{1,25},{9,1},{17,9},{25,17},{2,26},{10... | collective-permute-start | bytes 393224 | tf_op jit(solution)/shard_map/ppermute | solution.py:197
  21.8 50.2 %collective-permute-start.3 = (bf16[4,304,256]{2,1,0:T(8,128)(2,1)S(1)}, bf16[4,304,256]{2,1,0:T(8,128)(2,1)S(1)}, u32[]{:S(2)}, u32[]{:S(2)}) collective-permute-start(bf16[4,304,256]{2,1,0:T(8,128)(2,1)S(1)} %pad_maximum_fusion.lines_ref), channel_id=1, source_target_pairs={{0,1},{1,0},{2,3},{3,2},{4,5},{5,4},{6,7},{7,6},{8,9},{9,8},{10,11... | collective-permute-start | bytes 1867784 | tf_op jit(solution)/shard_map/ppermute | solution.py:202
  23.1 3.3 %collective-permute-start.4 = (s32[8,128]{1,0:T(8,128)S(1)}, s32[8,128]{1,0:T(8,128)S(1)}, u32[]{:S(2)}, u32[]{:S(2)}) collective-permute-start(s32[8,128]{1,0:T(8,128)S(1)} %broadcast_in_dim.8.refs_0_.own_ref), channel_id=1, source_target_pairs={{0,96},{32,0},{64,32},{96,64},{1,97},{33,1},{65,33},{97,65},{2,98}... | collective-permute-start | bytes 12296 | tf_op jit(solution)/shard_map/ppermute | solution.py:199
  26.4 3.9 %collective-permute-start.5 = (s32[8,128]{1,0:T(8,128)S(1)}, s32[8,128]{1,0:T(8,128)S(1)}, u32[]{:S(2)}, u32[]{:S(2)}) collective-permute-start(s32[8,128]{1,0:T(8,128)S(1)} %broadcast_in_dim.8.refs_0_.own_ref), channel_id=1, source_target_pairs={{0,32},{32,64},{64,96},{96,0},{1,33},{33,65},{65,97},{97,1},{2,34}... | collective-permute-start | bytes 12296 | tf_op jit(solution)/shard_map/ppermute | solution.py:199
  30.3 4.0 %collective-permute-start.6 = (s32[8,128]{1,0:T(8,128)S(1)}, s32[8,128]{1,0:T(8,128)S(1)}, u32[]{:S(2)}, u32[]{:S(2)}) collective-permute-start(s32[8,128]{1,0:T(8,128)S(1)} %broadcast_in_dim.8.refs_0_.own_ref), channel_id=1, source_target_pairs={{0,64},{32,96},{64,0},{96,32},{1,65},{33,97},{65,1},{97,33},{2,66}... | collective-permute-start | bytes 12296 | tf_op jit(solution)/shard_map/ppermute | solution.py:199
  34.3 5.6 %collective-permute-start.9 = (bf16[256,256]{1,0:T(8,128)(2,1)S(1)}, bf16[256,256]{1,0:T(8,128)(2,1)S(1)}, u32[]{:S(2)}, u32[]{:S(2)}) collective-permute-start(bf16[256,256]{1,0:T(8,128)(2,1)S(1)} %bitcast.14), channel_id=1, source_target_pairs={{0,16},{8,24},{16,0},{24,8},{1,17},{9,25},{17,1},{25,9},{2,18},{10... | collective-permute-start | bytes 393224 | tf_op jit(solution)/shard_map/ppermute | solution.py:197
  37.2 6.4 %collective-permute-start.11 = (bf16[256,256]{1,0:T(8,128)(2,1)S(1)}, bf16[256,256]{1,0:T(8,128)(2,1)S(1)}, u32[]{:S(2)}, u32[]{:S(2)}) collective-permute-start(bf16[256,256]{1,0:T(8,128)(2,1)S(1)} %collective-permute-done.10.refs_8_), channel_id=1, source_target_pairs={{0,8},{8,16},{16,24},{24,0},{1,9},{9,17},{17,25},{25,1},{2,10},{10... | collective-permute-start | bytes 393224 | tf_op jit(solution)/shard_map/ppermute | solution.py:198
  37.6 7.0 %collective-permute-start.12 = (bf16[256,256]{1,0:T(8,128)(2,1)S(1)}, bf16[256,256]{1,0:T(8,128)(2,1)S(1)}, u32[]{:S(2)}, u32[]{:S(2)}) collective-permute-start(bf16[256,256]{1,0:T(8,128)(2,1)S(1)} %collective-permute-done.10.refs_8_), channel_id=1, source_target_pairs={{0,24},{8,0},{16,8},{24,16},{1,25},{9,1},{17,9},{25,17},{2,26},{10... | collective-permute-start | bytes 393224 | tf_op jit(solution)/shard_map/ppermute | solution.py:198
  39.9 6.5 %collective-permute-start.13 = (bf16[256,256]{1,0:T(8,128)(2,1)S(1)}, bf16[256,256]{1,0:T(8,128)(2,1)S(1)}, u32[]{:S(2)}, u32[]{:S(2)}) collective-permute-start(bf16[256,256]{1,0:T(8,128)(2,1)S(1)} %collective-permute-done.10.refs_8_), channel_id=1, source_target_pairs={{0,16},{8,24},{16,0},{24,8},{1,17},{9,25},{17,1},{25,9},{2,18},{10... | collective-permute-start | bytes 393224 | tf_op jit(solution)/shard_map/ppermute | solution.py:198
  46.7 5.1 %collective-permute-start.14 = (bf16[256,256]{1,0:T(8,128)(2,1)S(1)}, bf16[256,256]{1,0:T(8,128)(2,1)S(1)}, u32[]{:S(2)}, u32[]{:S(2)}) collective-permute-start(bf16[256,256]{1,0:T(8,128)(2,1)S(1)} %get-tuple-element.18), channel_id=1, source_target_pairs={{0,32},{32,64},{64,96},{96,0},{1,33},{33,65},{65,97},{97,1},{2,34}... | collective-permute-start | bytes 393224 | tf_op jit(solution)/shard_map/ppermute | solution.py:204
  46.8 6.0 %collective-permute-start.15 = (bf16[256,256]{1,0:T(8,128)(2,1)S(1)}, bf16[256,256]{1,0:T(8,128)(2,1)S(1)}, u32[]{:S(2)}, u32[]{:S(2)}) collective-permute-start(bf16[256,256]{1,0:T(8,128)(2,1)S(1)} %get-tuple-element.19), channel_id=1, source_target_pairs={{0,96},{32,0},{64,32},{96,64},{1,97},{33,1},{65,33},{97,65},{2,98}... | collective-permute-start | bytes 393224 | tf_op jit(solution)/shard_map/ppermute | solution.py:204
  49.5 5.3 %collective-permute-start.16 = (bf16[256,256]{1,0:T(8,128)(2,1)S(1)}, bf16[256,256]{1,0:T(8,128)(2,1)S(1)}, u32[]{:S(2)}, u32[]{:S(2)}) collective-permute-start(bf16[256,256]{1,0:T(8,128)(2,1)S(1)} %get-tuple-element.20), channel_id=1, source_target_pairs={{0,64},{32,96},{64,0},{96,32},{1,65},{33,97},{65,1},{97,33},{2,66}... | collective-permute-start | bytes 393224 | tf_op jit(solution)/shard_map/ppermute | solution.py:204
  54.9 9.8 %collective-permute-start.19 = (bf16[256,256]{1,0:T(8,128)(2,1)S(1)}, bf16[256,256]{1,0:T(8,128)(2,1)S(1)}, u32[]{:S(2)}, u32[]{:S(2)}) collective-permute-start(bf16[256,256]{1,0:T(8,128)(2,1)S(1)} %shard_map.42.refs_0_), channel_id=1, source_target_pairs={{0,2},{2,4},{4,6},{6,0},{1,3},{3,5},{5,7},{7,1},{8,10},{10,12},{12... | collective-permute-start | bytes 393224 | tf_op jit(solution)/shard_map/ppermute | solution.py:207
  55.2 12.6 %collective-permute-start.20 = (bf16[256,256]{1,0:T(8,128)(2,1)S(1)}, bf16[256,256]{1,0:T(8,128)(2,1)S(1)}, u32[]{:S(2)}, u32[]{:S(2)}) collective-permute-start(bf16[256,256]{1,0:T(8,128)(2,1)S(1)} %shard_map.42.refs_0_), channel_id=1, source_target_pairs={{0,6},{2,0},{4,2},{6,4},{1,7},{3,1},{5,3},{7,5},{8,14},{10,8},{12,... | collective-permute-start | bytes 393224 | tf_op jit(solution)/shard_map/ppermute | solution.py:207
  58.5 9.7 %collective-permute-start.17 = (bf16[256,256]{1,0:T(8,128)(2,1)S(1)}, bf16[256,256]{1,0:T(8,128)(2,1)S(1)}, u32[]{:S(2)}, u32[]{:S(2)}) collective-permute-start(bf16[256,256]{1,0:T(8,128)(2,1)S(1)} %shard_map.42.refs_0_), channel_id=1, source_target_pairs={{0,4},{2,6},{4,0},{6,2},{1,5},{3,7},{5,1},{7,3},{8,12},{10,14},{12... | collective-permute-start | bytes 393224 | tf_op jit(solution)/shard_map/ppermute | solution.py:207
  58.5 13.5 %collective-permute-start.23 = (bf16[256,256]{1,0:T(8,128)(2,1)S(1)}, bf16[256,256]{1,0:T(8,128)(2,1)S(1)}, u32[]{:S(2)}, u32[]{:S(2)}) collective-permute-start(bf16[256,256]{1,0:T(8,128)(2,1)S(1)} %shard_map.42.refs_0_), channel_id=1, source_target_pairs={{0,1},{1,0},{2,3},{3,2},{4,5},{5,4},{6,7},{7,6},{8,9},{9,8},{10,11... | collective-permute-start | bytes 393224 | tf_op jit(solution)/shard_map/ppermute | solution.py:208
  64.7 8.3 %collective-permute-start.21 = (bf16[256,256]{1,0:T(8,128)(2,1)S(1)}, bf16[256,256]{1,0:T(8,128)(2,1)S(1)}, u32[]{:S(2)}, u32[]{:S(2)}) collective-permute-start(bf16[256,256]{1,0:T(8,128)(2,1)S(1)} %collective-permute-done.19.refs_0_), channel_id=1, source_target_pairs={{0,1},{1,0},{2,3},{3,2},{4,5},{5,4},{6,7},{7,6},{8,9},{9,8},{10,11... | collective-permute-start | bytes 393224 | tf_op jit(solution)/shard_map/ppermute | solution.py:208
  67.8 5.3 %collective-permute-start.22 = (bf16[256,256]{1,0:T(8,128)(2,1)S(1)}, bf16[256,256]{1,0:T(8,128)(2,1)S(1)}, u32[]{:S(2)}, u32[]{:S(2)}) collective-permute-start(bf16[256,256]{1,0:T(8,128)(2,1)S(1)} %collective-permute-done.20.refs_1_), channel_id=1, source_target_pairs={{0,1},{1,0},{2,3},{3,2},{4,5},{5,4},{6,7},{7,6},{8,9},{9,8},{10,11... | collective-permute-start | bytes 393224 | tf_op jit(solution)/shard_map/ppermute | solution.py:208
  68.2 6.9 %collective-permute-start.18 = (bf16[256,256]{1,0:T(8,128)(2,1)S(1)}, bf16[256,256]{1,0:T(8,128)(2,1)S(1)}, u32[]{:S(2)}, u32[]{:S(2)}) collective-permute-start(bf16[256,256]{1,0:T(8,128)(2,1)S(1)} %collective-permute-done.17.refs_0_), channel_id=1, source_target_pairs={{0,1},{1,0},{2,3},{3,2},{4,5},{5,4},{6,7},{7,6},{8,9},{9,8},{10,11... | collective-permute-start | bytes 393224 | tf_op jit(solution)/shard_map/ppermute | solution.py:208

commit v4 on v3

--- a/solution.py
+++ b/solution.py
@@ -95,9 +95,8 @@
     )(own, *came)
 
 
-def couple(kq, lines, twins, others, steps, bands, modes, last, before=None):
+def couple(kq, lines, twins, others, pieces, bands, modes, last, before=None):
     parts = len(others)
-    half = parts // 2
     cells = others[0].shape[1]
     wide = parts * cells
     rows = 2 * bands
@@ -120,11 +119,11 @@
         crossed = kq_ref[0] // 16 != lax.axis_index("zh")
         for p in range(parts):
             at = slice(p * cells, (p + 1) * cells)
-            s = steps[p % half]
+            s, twin = pieces[p]
             turned = lax.rem(2 * zl + 5 - s, 4)
             turned = jnp.where(turned == 2, 3, jnp.where(turned == 3, 2, turned))
             index = jnp.where(crossed, turned, STEPS.index(s))
-            source = lines_ref if p < half else twins_ref
+            source = twins_ref if twin else lines_ref
             wave_re[:, at] = source[index, :bands].astype(jnp.float32)
             wave_im[:, at] = source[index, bands:rows].astype(jnp.float32)
             pots[:, at] = source[index, rows:].astype(jnp.float32)
@@ -198,17 +197,23 @@
     far = [swapped] + [lax.ppermute(swapped, "y", ring(STEPS[i])) for i in (1, 2, 3)]
     wanted = [tag] + [lax.ppermute(tag, "x", ring(-STEPS[i])) for i in (1, 2, 3)]
     lines = [packs[0]] + [lax.ppermute(packs[i], "zl", ring(STEPS[i])) for i in (1, 2, 3)]
-    lines = jnp.stack(lines)
-    twins = lax.ppermute(lines, "c", SWAP)
     slots = choose(wanted, near + far)
     came = [slots[0]] + [lax.ppermute(slots[i], "x", ring(STEPS[i])) for i in (1, 2, 3)]
     phi = keep(tag, came)
+    lines = jnp.stack(lines)
+    twins = lax.ppermute(lines, "c", SWAP)
 
     others = [phi] + [lax.ppermute(phi, "zl", ring(STEPS[i])) for i in (1, 2, 3)]
     mates = [lax.ppermute(o, "c", SWAP) for o in others]
     out = None
-    for name, at in (("early", slice(0, 1)), ("middle", slice(1, 3)), ("late", slice(3, 4))):
-        out = couple(kq_map, lines, twins, others[at] + mates[at], STEPS[at], bands, modes, name == "late", out)
+    for name, values, pieces in (
+        ("early", (others[0], mates[0]), ((0, False), (0, True))),
+        ("middle", others[1:3], ((1, False), (3, False))),
+        ("paired", mates[1:3], ((1, True), (3, True))),
+        ("final", others[3:], ((2, False),)),
+        ("last", mates[3:], ((2, True),)),
+    ):
+        out = couple(kq_map, lines, twins, values, pieces, bands, modes, name == "last", out)
     return out[:, None]
 
 

time: 77.3 us -> 78.1 us (1.010)
    pallas_call x3 -> x5, Pallas kernels: 5.02 us -> 5.8 us  [couple(): pl.pallas_call(kernel, in_specs=specs, out_specs=pl.BlockSpec(memory_spac...]
  transfers between devices with their start and end apart: 24 -> 24, of which waited for: 10 -> 10; matrix products, arithmetic and copies ran while one was open for 0% -> 0% of each run, Pallas kernels for 5% -> 6%
where the time goes in v4:
time: 78.1 us; the launch traced here: 77.9 us
  starting transfers between devices  41.7 us (53%)
  waiting for transfers between devices  27 us (35%)
  Pallas kernels  6.39 us (8%)
  local copies, waits for them, and re-layouts  1.8 us (2%)
  between operations  0.93 us (1%)
    ppermute x4, starting transfers between devices, body(): mates = [lax.ppermute(o, 'c', SWAP) for o in others]  13.4 us
    ppermute x3, waiting for transfers between devices, body(): lax.ppermute(packs[i], 'zl', ring(STEPS[i]))  7.92 us
    ppermute x3, waiting for transfers between devices, body(): lax.ppermute(tag, 'x', ring(-STEPS[i]))  7.25 us
    ppermute x3, waiting for transfers between devices, body(): lax.ppermute(swapped, 'y', ring(STEPS[i]))  6.5 us
    pallas_call x5, Pallas kernels, couple(): pl.pallas_call(kernel, in_specs=specs, out_specs=pl.BlockSpec(memory_spac...  5.8 us
    ppermute x3, starting transfers between devices, body(): near = [slab] + [lax.ppermute(slab, 'y', ring(STEPS[i])) for i in (1, 2, 3)]  5.66 us
    ppermute x3, starting transfers between devices, body(): lax.ppermute(packs[i], 'zl', ring(STEPS[i]))  5.53 us
    ppermute x3, waiting for transfers between devices, body(): lax.ppermute(slots[i], 'x', ring(STEPS[i]))  5.32 us
  transfers between devices with their start and end apart: 24, of which 10 were waited for; matrix products, arithmetic and copies ran while one was open for 0% of the time, Pallas kernels for 6%

profile of v4, /device:TPU:1, one launch (start us, length us, event | category | flops | bytes accessed | tf_op | source)
XLA Modules:
  0.0 77.9 jit_solution(922776414620379790)
XLA Ops:
  0.0 0.9 %copy-done = bf16[1,2,128,256]{3,2,1,0:T(8,128)(2,1)S(1)} copy-done((bf16[1,2,128,256]{3,2,1,0:T(8,128)(2,1)S(1)}, bf16[1,2,128,256]{3,2,1,0:T(8,128)(2,1)}, u32[]{:S(2)}) %copy-start) | copy-done | bytes 131096
  0.9 0.9 %copy-done.1 = bf16[96,2,256]{2,1,0:T(2,128)(2,1)S(1)} copy-done((bf16[96,2,256]{2,1,0:T(2,128)(2,1)S(1)}, bf16[96,2,256]{2,1,0:T(2,128)(2,1)}, u32[]{:S(2)}) %copy-start.1) | copy-done | bytes 98328
  1.9 2.5 %collective-permute-start = (bf16[304,256]{1,0:T(8,128)(2,1)S(1)}, bf16[304,256]{1,0:T(8,128)(2,1)S(1)}, u32[]{:S(2)}, u32[]{:S(2)}) collective-permute-start(bf16[304,256]{1,0:T(8,128)(2,1)S(1)} %get-tuple-element.14), channel_id=1, source_target_pairs={{0,2},{2,4},{4,6},{6,0},{1,3},{3,5},{5,7},{7,1},{8,10},{10,12},{12... | collective-permute-start | bytes 466952 | tf_op jit(solution)/shard_map/ppermute | solution.py:199
  4.4 2.8 %collective-permute-start.1 = (bf16[304,256]{1,0:T(8,128)(2,1)S(1)}, bf16[304,256]{1,0:T(8,128)(2,1)S(1)}, u32[]{:S(2)}, u32[]{:S(2)}) collective-permute-start(bf16[304,256]{1,0:T(8,128)(2,1)S(1)} %get-tuple-element.15), channel_id=1, source_target_pairs={{0,6},{2,0},{4,2},{6,4},{1,7},{3,1},{5,3},{7,5},{8,14},{10,8},{12,... | collective-permute-start | bytes 466952 | tf_op jit(solution)/shard_map/ppermute | solution.py:199
  7.4 3.6 %collective-permute-start.10 = (bf16[256,256]{1,0:T(8,128)(2,1)S(1)}, bf16[256,256]{1,0:T(8,128)(2,1)S(1)}, u32[]{:S(2)}, u32[]{:S(2)}) collective-permute-start(bf16[256,256]{1,0:T(8,128)(2,1)S(1)} %bitcast.11), channel_id=1, source_target_pairs={{0,134},{2,132},{4,130},{6,128},{128,6},{130,4},{132,2},{134,0},{1... | collective-permute-start | bytes 393224 | tf_op jit(solution)/shard_map/ppermute | solution.py:193
  11.0 1.3 %collective-permute-start.7 = (bf16[256,256]{1,0:T(8,128)(2,1)S(1)}, bf16[256,256]{1,0:T(8,128)(2,1)S(1)}, u32[]{:S(2)}, u32[]{:S(2)}) collective-permute-start(bf16[256,256]{1,0:T(8,128)(2,1)S(1)} %bitcast.12), channel_id=1, source_target_pairs={{0,8},{8,16},{16,24},{24,0},{1,9},{9,17},{17,25},{25,1},{2,10},{10... | collective-permute-start | bytes 393224 | tf_op jit(solution)/shard_map/ppermute | solution.py:196
  12.3 1.4 %collective-permute-start.8 = (bf16[256,256]{1,0:T(8,128)(2,1)S(1)}, bf16[256,256]{1,0:T(8,128)(2,1)S(1)}, u32[]{:S(2)}, u32[]{:S(2)}) collective-permute-start(bf16[256,256]{1,0:T(8,128)(2,1)S(1)} %bitcast.13), channel_id=1, source_target_pairs={{0,24},{8,0},{16,8},{24,16},{1,25},{9,1},{17,9},{25,17},{2,26},{10... | collective-permute-start | bytes 393224 | tf_op jit(solution)/shard_map/ppermute | solution.py:196
  13.8 7.9 %collective-permute-done.2 = bf16[304,256]{1,0:T(8,128)(2,1)S(1)} collective-permute-done((bf16[304,256]{1,0:T(8,128)(2,1)S(1)}, bf16[304,256]{1,0:T(8,128)(2,1)S(1)}, u32[]{:S(2)}, u32[]{:S(2)}) %collective-permute-start.2) | collective-permute-done | bytes 155680 | tf_op jit(solution)/shard_map/ppermute | solution.py:199
  21.8 0.6 collective-permute-start.3
  23.1 2.6 %collective-permute-start.4 = (s32[8,128]{1,0:T(8,128)S(1)}, s32[8,128]{1,0:T(8,128)S(1)}, u32[]{:S(2)}, u32[]{:S(2)}) collective-permute-start(s32[8,128]{1,0:T(8,128)S(1)} %broadcast_in_dim.8.refs_0_.own_ref), channel_id=1, source_target_pairs={{0,96},{32,0},{64,32},{96,64},{1,97},{33,1},{65,33},{97,65},{2,98}... | collective-permute-start | bytes 12296 | tf_op jit(solution)/shard_map/ppermute | solution.py:198
  25.6 0.8 collective-permute-done.4.refs_1_
  26.8 3.5 %collective-permute-done.5.refs_2_ = s32[8,128]{1,0:T(8,128)S(1)} collective-permute-done((s32[8,128]{1,0:T(8,128)S(1)}, s32[8,128]{1,0:T(8,128)S(1)}, u32[]{:S(2)}, u32[]{:S(2)}) %collective-permute-start.5) | collective-permute-done | bytes 4128 | tf_op jit(solution)/shard_map/ppermute | solution.py:198
  30.3 0.9 %collective-permute-start.6 = (s32[8,128]{1,0:T(8,128)S(1)}, s32[8,128]{1,0:T(8,128)S(1)}, u32[]{:S(2)}, u32[]{:S(2)}) collective-permute-start(s32[8,128]{1,0:T(8,128)S(1)} %broadcast_in_dim.8.refs_0_.own_ref), channel_id=1, source_target_pairs={{0,64},{32,96},{64,0},{96,32},{1,65},{33,97},{65,1},{97,33},{2,66}... | collective-permute-start | bytes 12296 | tf_op jit(solution)/shard_map/ppermute | solution.py:198
  31.2 3.0 %collective-permute-done.6.refs_3_ = s32[8,128]{1,0:T(8,128)S(1)} collective-permute-done((s32[8,128]{1,0:T(8,128)S(1)}, s32[8,128]{1,0:T(8,128)S(1)}, u32[]{:S(2)}, u32[]{:S(2)}) %collective-permute-start.6) | collective-permute-done | bytes 4128 | tf_op jit(solution)/shard_map/ppermute | solution.py:198
  34.3 2.9 %collective-permute-start.9 = (bf16[256,256]{1,0:T(8,128)(2,1)S(1)}, bf16[256,256]{1,0:T(8,128)(2,1)S(1)}, u32[]{:S(2)}, u32[]{:S(2)}) collective-permute-start(bf16[256,256]{1,0:T(8,128)(2,1)S(1)} %bitcast.14), channel_id=1, source_target_pairs={{0,16},{8,24},{16,0},{24,8},{1,17},{9,25},{17,1},{25,9},{2,18},{10... | collective-permute-start | bytes 393224 | tf_op jit(solution)/shard_map/ppermute | solution.py:196
  37.6 2.3 %collective-permute-start.12 = (bf16[256,256]{1,0:T(8,128)(2,1)S(1)}, bf16[256,256]{1,0:T(8,128)(2,1)S(1)}, u32[]{:S(2)}, u32[]{:S(2)}) collective-permute-start(bf16[256,256]{1,0:T(8,128)(2,1)S(1)} %collective-permute-done.10.refs_8_), channel_id=1, source_target_pairs={{0,24},{8,0},{16,8},{24,16},{1,25},{9,1},{17,9},{25,17},{2,26},{10... | collective-permute-start | bytes 393224 | tf_op jit(solution)/shard_map/ppermute | solution.py:197
  39.9 3.7 %collective-permute-done.11.refs_9_ = bf16[256,256]{1,0:T(8,128)(2,1)S(1)} collective-permute-done((bf16[256,256]{1,0:T(8,128)(2,1)S(1)}, bf16[256,256]{1,0:T(8,128)(2,1)S(1)}, u32[]{:S(2)}, u32[]{:S(2)}) %collective-permute-start.11) | collective-permute-done | bytes 131104 | tf_op jit(solution)/shard_map/ppermute | solution.py:197
  43.6 1.0 %collective-permute-done.12.refs_10_ = bf16[256,256]{1,0:T(8,128)(2,1)S(1)} collective-permute-done((bf16[256,256]{1,0:T(8,128)(2,1)S(1)}, bf16[256,256]{1,0:T(8,128)(2,1)S(1)}, u32[]{:S(2)}, u32[]{:S(2)}) %collective-permute-start.12) | collective-permute-done | bytes 131104 | tf_op jit(solution)/shard_map/ppermute | solution.py:197
  44.6 1.8 %collective-permute-done.13.refs_11_ = bf16[256,256]{1,0:T(8,128)(2,1)S(1)} collective-permute-done((bf16[256,256]{1,0:T(8,128)(2,1)S(1)}, bf16[256,256]{1,0:T(8,128)(2,1)S(1)}, u32[]{:S(2)}, u32[]{:S(2)}) %collective-permute-start.13) | collective-permute-done | bytes 131104 | tf_op jit(solution)/shard_map/ppermute | solution.py:197
  46.8 2.7 %collective-permute-start.15 = (bf16[256,256]{1,0:T(8,128)(2,1)S(1)}, bf16[256,256]{1,0:T(8,128)(2,1)S(1)}, u32[]{:S(2)}, u32[]{:S(2)}) collective-permute-start(bf16[256,256]{1,0:T(8,128)(2,1)S(1)} %get-tuple-element.19), channel_id=1, source_target_pairs={{0,96},{32,0},{64,32},{96,64},{1,97},{33,1},{65,33},{97,65},{2,98}... | collective-permute-start | bytes 393224 | tf_op jit(solution)/shard_map/ppermute | solution.py:201
  49.5 2.3 %collective-permute-done.14.refs_1_ = bf16[256,256]{1,0:T(8,128)(2,1)S(1)} collective-permute-done((bf16[256,256]{1,0:T(8,128)(2,1)S(1)}, bf16[256,256]{1,0:T(8,128)(2,1)S(1)}, u32[]{:S(2)}, u32[]{:S(2)}) %collective-permute-start.14) | collective-permute-done | bytes 131104 | tf_op jit(solution)/shard_map/ppermute | solution.py:201
  51.8 1.0 %collective-permute-done.15.refs_2_ = bf16[256,256]{1,0:T(8,128)(2,1)S(1)} collective-permute-done((bf16[256,256]{1,0:T(8,128)(2,1)S(1)}, bf16[256,256]{1,0:T(8,128)(2,1)S(1)}, u32[]{:S(2)}, u32[]{:S(2)}) %collective-permute-start.15) | collective-permute-done | bytes 131104 | tf_op jit(solution)/shard_map/ppermute | solution.py:201
  52.8 2.0 %collective-permute-done.16.refs_3_ = bf16[256,256]{1,0:T(8,128)(2,1)S(1)} collective-permute-done((bf16[256,256]{1,0:T(8,128)(2,1)S(1)}, bf16[256,256]{1,0:T(8,128)(2,1)S(1)}, u32[]{:S(2)}, u32[]{:S(2)}) %collective-permute-start.16) | collective-permute-done | bytes 131104 | tf_op jit(solution)/shard_map/ppermute | solution.py:201
  55.2 3.3 %collective-permute-start.21 = (bf16[256,256]{1,0:T(8,128)(2,1)S(1)}, bf16[256,256]{1,0:T(8,128)(2,1)S(1)}, u32[]{:S(2)}, u32[]{:S(2)}) collective-permute-start(bf16[256,256]{1,0:T(8,128)(2,1)S(1)} %shard_map.42.refs_0_), channel_id=1, source_target_pairs={{0,6},{2,0},{4,2},{6,4},{1,7},{3,1},{5,3},{7,5},{8,14},{10,8},{12,... | collective-permute-start | bytes 393224 | tf_op jit(solution)/shard_map/ppermute | solution.py:206
  58.5 6.3 %collective-permute-start.23 = (bf16[256,256]{1,0:T(8,128)(2,1)S(1)}, bf16[256,256]{1,0:T(8,128)(2,1)S(1)}, u32[]{:S(2)}, u32[]{:S(2)}) collective-permute-start(bf16[256,256]{1,0:T(8,128)(2,1)S(1)} %shard_map.42.refs_0_), channel_id=1, source_target_pairs={{0,1},{1,0},{2,3},{3,2},{4,5},{5,4},{6,7},{7,6},{8,9},{9,8},{10,11... | collective-permute-start | bytes 393224 | tf_op jit(solution)/shard_map/ppermute | solution.py:207
  64.7 3.0 %collective-permute-start.20 = (bf16[256,256]{1,0:T(8,128)(2,1)S(1)}, bf16[256,256]{1,0:T(8,128)(2,1)S(1)}, u32[]{:S(2)}, u32[]{:S(2)}) collective-permute-start(bf16[256,256]{1,0:T(8,128)(2,1)S(1)} %collective-permute-done.19.refs_0_), channel_id=1, source_target_pairs={{0,1},{1,0},{2,3},{3,2},{4,5},{5,4},{6,7},{7,6},{8,9},{9,8},{10,11... | collective-permute-start | bytes 393224 | tf_op jit(solution)/shard_map/ppermute | solution.py:207
  68.2 3.8 %collective-permute-start.18 = (bf16[256,256]{1,0:T(8,128)(2,1)S(1)}, bf16[256,256]{1,0:T(8,128)(2,1)S(1)}, u32[]{:S(2)}, u32[]{:S(2)}) collective-permute-start(bf16[256,256]{1,0:T(8,128)(2,1)S(1)} %collective-permute-done.17.refs_0_), channel_id=1, source_target_pairs={{0,1},{1,0},{2,3},{3,2},{4,5},{5,4},{6,7},{7,6},{8,9},{9,8},{10,11... | collective-permute-start | bytes 393224 | tf_op jit(solution)/shard_map/ppermute | solution.py:207
  71.9 1.1 %shard_map.43.refs_2_ = f32[12,2,128,128]{3,2,1,0:T(8,128)S(1)} custom-call(s32[1]{0:T(128)} %copy.5.kq_ref, bf16[4,304,256]{2,1,0:T(8,128)(2,1)S(1)} %pad_maximum_fusion.lines_ref, bf16[4,304,256]{2,1,0:T(8,128)(2,1)S(1)} %collective-permute-done.3.twins_ref, bf16[256,256]{1,0:T(8,128)(2,1)S(1)} %shard_map.42.refs_0_, ...), custom_call_target="tpu_custom_call" | custom-call | tf_op jit(solution)/shard_map/pallas_call | solution.py:178
  73.1 1.2 %shard_map.44.refs_2_ = f32[12,2,128,128]{3,2,1,0:T(8,128)S(1)} custom-call(s32[1]{0:T(128)} %copy.5.kq_ref, bf16[4,304,256]{2,1,0:T(8,128)(2,1)S(1)} %pad_maximum_fusion.lines_ref, bf16[4,304,256]{2,1,0:T(8,128)(2,1)S(1)} %collective-permute-done.3.twins_ref, bf16[256,256]{1,0:T(8,128)(2,1)S(1)} %collective-permute-done.19.refs_0_, ...), custom_call_target="tpu_custom_call" | custom-call | tf_op jit(solution)/shard_map/pallas_call | solution.py:178
  74.3 1.2 %shard_map.45.refs_1_ = f32[12,2,128,128]{3,2,1,0:T(8,128)S(1)} custom-call(s32[1]{0:T(128)} %copy.5.kq_ref, bf16[4,304,256]{2,1,0:T(8,128)(2,1)S(1)} %pad_maximum_fusion.lines_ref, bf16[4,304,256]{2,1,0:T(8,128)(2,1)S(1)} %collective-permute-done.3.twins_ref, bf16[256,256]{1,0:T(8,128)(2,1)S(1)} %collective-permute-done.20.refs_0_, ...), custom_call_target="tpu_custom_call" | custom-call | tf_op jit(solution)/shard_map/pallas_call | solution.py:178
  75.5 0.7 shard_map.46.refs_1_
  76.2 1.5 %shard_map.47 = f32[12,2,128,128]{3,2,1,0:T(8,128)} custom-call(s32[1]{0:T(128)} %copy.5.kq_ref, bf16[4,304,256]{2,1,0:T(8,128)(2,1)S(1)} %pad_maximum_fusion.lines_ref, bf16[4,304,256]{2,1,0:T(8,128)(2,1)S(1)} %collective-permute-done.3.twins_ref, bf16[256,256]{1,0:T(8,128)(2,1)S(1)} %collective-permute-done.18.refs_0_, ...), custom_call_target="tpu_custom_call" | custom-call | tf_op jit(solution)/shard_map/pallas_call | solution.py:178
  (30 shorter events, 2.5 us)
Async XLA Ops:
  0.0 0.9 %copy-start = (bf16[1,2,128,256]{3,2,1,0:T(8,128)(2,1)S(1)}, bf16[1,2,128,256]{3,2,1,0:T(8,128)(2,1)}, u32[]{:S(2)}) copy-start(bf16[1,2,128,256]{3,2,1,0:T(8,128)(2,1)} %param.3) | copy-start | bytes 393220
  0.9 0.9 %copy-start.1 = (bf16[96,2,256]{2,1,0:T(2,128)(2,1)S(1)}, bf16[96,2,256]{2,1,0:T(2,128)(2,1)}, u32[]{:S(2)}) copy-start(bf16[96,2,256]{2,1,0:T(2,128)(2,1)} %pot_ref.1) | copy-start | bytes 294916
  1.9 10.4 %collective-permute-start = (bf16[304,256]{1,0:T(8,128)(2,1)S(1)}, bf16[304,256]{1,0:T(8,128)(2,1)S(1)}, u32[]{:S(2)}, u32[]{:S(2)}) collective-permute-start(bf16[304,256]{1,0:T(8,128)(2,1)S(1)} %get-tuple-element.14), channel_id=1, source_target_pairs={{0,2},{2,4},{4,6},{6,0},{1,3},{3,5},{5,7},{7,1},{8,10},{10,12},{12... | collective-permute-start | bytes 466952 | tf_op jit(solution)/shard_map/ppermute | solution.py:199
  4.4 9.3 %collective-permute-start.1 = (bf16[304,256]{1,0:T(8,128)(2,1)S(1)}, bf16[304,256]{1,0:T(8,128)(2,1)S(1)}, u32[]{:S(2)}, u32[]{:S(2)}) collective-permute-start(bf16[304,256]{1,0:T(8,128)(2,1)S(1)} %get-tuple-element.15), channel_id=1, source_target_pairs={{0,6},{2,0},{4,2},{6,4},{1,7},{3,1},{5,3},{7,5},{8,14},{10,8},{12,... | collective-permute-start | bytes 466952 | tf_op jit(solution)/shard_map/ppermute | solution.py:199
  7.2 14.4 %collective-permute-start.2 = (bf16[304,256]{1,0:T(8,128)(2,1)S(1)}, bf16[304,256]{1,0:T(8,128)(2,1)S(1)}, u32[]{:S(2)}, u32[]{:S(2)}) collective-permute-start(bf16[304,256]{1,0:T(8,128)(2,1)S(1)} %get-tuple-element.16), channel_id=1, source_target_pairs={{0,4},{2,6},{4,0},{6,2},{1,5},{3,7},{5,1},{7,3},{8,12},{10,14},{12... | collective-permute-start | bytes 466952 | tf_op jit(solution)/shard_map/ppermute | solution.py:199
  7.4 29.7 %collective-permute-start.10 = (bf16[256,256]{1,0:T(8,128)(2,1)S(1)}, bf16[256,256]{1,0:T(8,128)(2,1)S(1)}, u32[]{:S(2)}, u32[]{:S(2)}) collective-permute-start(bf16[256,256]{1,0:T(8,128)(2,1)S(1)} %bitcast.11), channel_id=1, source_target_pairs={{0,134},{2,132},{4,130},{6,128},{128,6},{130,4},{132,2},{134,0},{1... | collective-permute-start | bytes 393224 | tf_op jit(solution)/shard_map/ppermute | solution.py:193
  11.0 26.6 %collective-permute-start.7 = (bf16[256,256]{1,0:T(8,128)(2,1)S(1)}, bf16[256,256]{1,0:T(8,128)(2,1)S(1)}, u32[]{:S(2)}, u32[]{:S(2)}) collective-permute-start(bf16[256,256]{1,0:T(8,128)(2,1)S(1)} %bitcast.12), channel_id=1, source_target_pairs={{0,8},{8,16},{16,24},{24,0},{1,9},{9,17},{17,25},{25,1},{2,10},{10... | collective-permute-start | bytes 393224 | tf_op jit(solution)/shard_map/ppermute | solution.py:196
  12.3 27.5 %collective-permute-start.8 = (bf16[256,256]{1,0:T(8,128)(2,1)S(1)}, bf16[256,256]{1,0:T(8,128)(2,1)S(1)}, u32[]{:S(2)}, u32[]{:S(2)}) collective-permute-start(bf16[256,256]{1,0:T(8,128)(2,1)S(1)} %bitcast.13), channel_id=1, source_target_pairs={{0,24},{8,0},{16,8},{24,16},{1,25},{9,1},{17,9},{25,17},{2,26},{10... | collective-permute-start | bytes 393224 | tf_op jit(solution)/shard_map/ppermute | solution.py:196
  21.8 50.2 %collective-permute-start.3 = (bf16[4,304,256]{2,1,0:T(8,128)(2,1)S(1)}, bf16[4,304,256]{2,1,0:T(8,128)(2,1)S(1)}, u32[]{:S(2)}, u32[]{:S(2)}) collective-permute-start(bf16[4,304,256]{2,1,0:T(8,128)(2,1)S(1)} %pad_maximum_fusion.lines_ref), channel_id=1, source_target_pairs={{0,1},{1,0},{2,3},{3,2},{4,5},{5,4},{6,7},{7,6},{8,9},{9,8},{10,11... | collective-permute-start | bytes 1867784 | tf_op jit(solution)/shard_map/ppermute | solution.py:204
  23.1 3.3 %collective-permute-start.4 = (s32[8,128]{1,0:T(8,128)S(1)}, s32[8,128]{1,0:T(8,128)S(1)}, u32[]{:S(2)}, u32[]{:S(2)}) collective-permute-start(s32[8,128]{1,0:T(8,128)S(1)} %broadcast_in_dim.8.refs_0_.own_ref), channel_id=1, source_target_pairs={{0,96},{32,0},{64,32},{96,64},{1,97},{33,1},{65,33},{97,65},{2,98}... | collective-permute-start | bytes 12296 | tf_op jit(solution)/shard_map/ppermute | solution.py:198
  26.4 3.9 %collective-permute-start.5 = (s32[8,128]{1,0:T(8,128)S(1)}, s32[8,128]{1,0:T(8,128)S(1)}, u32[]{:S(2)}, u32[]{:S(2)}) collective-permute-start(s32[8,128]{1,0:T(8,128)S(1)} %broadcast_in_dim.8.refs_0_.own_ref), channel_id=1, source_target_pairs={{0,32},{32,64},{64,96},{96,0},{1,33},{33,65},{65,97},{97,1},{2,34}... | collective-permute-start | bytes 12296 | tf_op jit(solution)/shard_map/ppermute | solution.py:198
  30.3 4.0 %collective-permute-start.6 = (s32[8,128]{1,0:T(8,128)S(1)}, s32[8,128]{1,0:T(8,128)S(1)}, u32[]{:S(2)}, u32[]{:S(2)}) collective-permute-start(s32[8,128]{1,0:T(8,128)S(1)} %broadcast_in_dim.8.refs_0_.own_ref), channel_id=1, source_target_pairs={{0,64},{32,96},{64,0},{96,32},{1,65},{33,97},{65,1},{97,33},{2,66}... | collective-permute-start | bytes 12296 | tf_op jit(solution)/shard_map/ppermute | solution.py:198
  34.3 5.6 %collective-permute-start.9 = (bf16[256,256]{1,0:T(8,128)(2,1)S(1)}, bf16[256,256]{1,0:T(8,128)(2,1)S(1)}, u32[]{:S(2)}, u32[]{:S(2)}) collective-permute-start(bf16[256,256]{1,0:T(8,128)(2,1)S(1)} %bitcast.14), channel_id=1, source_target_pairs={{0,16},{8,24},{16,0},{24,8},{1,17},{9,25},{17,1},{25,9},{2,18},{10... | collective-permute-start | bytes 393224 | tf_op jit(solution)/shard_map/ppermute | solution.py:196
  37.2 6.4 %collective-permute-start.11 = (bf16[256,256]{1,0:T(8,128)(2,1)S(1)}, bf16[256,256]{1,0:T(8,128)(2,1)S(1)}, u32[]{:S(2)}, u32[]{:S(2)}) collective-permute-start(bf16[256,256]{1,0:T(8,128)(2,1)S(1)} %collective-permute-done.10.refs_8_), channel_id=1, source_target_pairs={{0,8},{8,16},{16,24},{24,0},{1,9},{9,17},{17,25},{25,1},{2,10},{10... | collective-permute-start | bytes 393224 | tf_op jit(solution)/shard_map/ppermute | solution.py:197
  37.6 7.0 %collective-permute-start.12 = (bf16[256,256]{1,0:T(8,128)(2,1)S(1)}, bf16[256,256]{1,0:T(8,128)(2,1)S(1)}, u32[]{:S(2)}, u32[]{:S(2)}) collective-permute-start(bf16[256,256]{1,0:T(8,128)(2,1)S(1)} %collective-permute-done.10.refs_8_), channel_id=1, source_target_pairs={{0,24},{8,0},{16,8},{24,16},{1,25},{9,1},{17,9},{25,17},{2,26},{10... | collective-permute-start | bytes 393224 | tf_op jit(solution)/shard_map/ppermute | solution.py:197
  39.9 6.5 %collective-permute-start.13 = (bf16[256,256]{1,0:T(8,128)(2,1)S(1)}, bf16[256,256]{1,0:T(8,128)(2,1)S(1)}, u32[]{:S(2)}, u32[]{:S(2)}) collective-permute-start(bf16[256,256]{1,0:T(8,128)(2,1)S(1)} %collective-permute-done.10.refs_8_), channel_id=1, source_target_pairs={{0,16},{8,24},{16,0},{24,8},{1,17},{9,25},{17,1},{25,9},{2,18},{10... | collective-permute-start | bytes 393224 | tf_op jit(solution)/shard_map/ppermute | solution.py:197
  46.7 5.1 %collective-permute-start.14 = (bf16[256,256]{1,0:T(8,128)(2,1)S(1)}, bf16[256,256]{1,0:T(8,128)(2,1)S(1)}, u32[]{:S(2)}, u32[]{:S(2)}) collective-permute-start(bf16[256,256]{1,0:T(8,128)(2,1)S(1)} %get-tuple-element.18), channel_id=1, source_target_pairs={{0,32},{32,64},{64,96},{96,0},{1,33},{33,65},{65,97},{97,1},{2,34}... | collective-permute-start | bytes 393224 | tf_op jit(solution)/shard_map/ppermute | solution.py:201
  46.8 6.0 %collective-permute-start.15 = (bf16[256,256]{1,0:T(8,128)(2,1)S(1)}, bf16[256,256]{1,0:T(8,128)(2,1)S(1)}, u32[]{:S(2)}, u32[]{:S(2)}) collective-permute-start(bf16[256,256]{1,0:T(8,128)(2,1)S(1)} %get-tuple-element.19), channel_id=1, source_target_pairs={{0,96},{32,0},{64,32},{96,64},{1,97},{33,1},{65,33},{97,65},{2,98}... | collective-permute-start | bytes 393224 | tf_op jit(solution)/shard_map/ppermute | solution.py:201
  49.5 5.3 %collective-permute-start.16 = (bf16[256,256]{1,0:T(8,128)(2,1)S(1)}, bf16[256,256]{1,0:T(8,128)(2,1)S(1)}, u32[]{:S(2)}, u32[]{:S(2)}) collective-permute-start(bf16[256,256]{1,0:T(8,128)(2,1)S(1)} %get-tuple-element.20), channel_id=1, source_target_pairs={{0,64},{32,96},{64,0},{96,32},{1,65},{33,97},{65,1},{97,33},{2,66}... | collective-permute-start | bytes 393224 | tf_op jit(solution)/shard_map/ppermute | solution.py:201
  54.9 9.8 %collective-permute-start.19 = (bf16[256,256]{1,0:T(8,128)(2,1)S(1)}, bf16[256,256]{1,0:T(8,128)(2,1)S(1)}, u32[]{:S(2)}, u32[]{:S(2)}) collective-permute-start(bf16[256,256]{1,0:T(8,128)(2,1)S(1)} %shard_map.42.refs_0_), channel_id=1, source_target_pairs={{0,2},{2,4},{4,6},{6,0},{1,3},{3,5},{5,7},{7,1},{8,10},{10,12},{12... | collective-permute-start | bytes 393224 | tf_op jit(solution)/shard_map/ppermute | solution.py:206
  55.2 12.6 %collective-permute-start.21 = (bf16[256,256]{1,0:T(8,128)(2,1)S(1)}, bf16[256,256]{1,0:T(8,128)(2,1)S(1)}, u32[]{:S(2)}, u32[]{:S(2)}) collective-permute-start(bf16[256,256]{1,0:T(8,128)(2,1)S(1)} %shard_map.42.refs_0_), channel_id=1, source_target_pairs={{0,6},{2,0},{4,2},{6,4},{1,7},{3,1},{5,3},{7,5},{8,14},{10,8},{12,... | collective-permute-start | bytes 393224 | tf_op jit(solution)/shard_map/ppermute | solution.py:206
  58.5 9.7 %collective-permute-start.17 = (bf16[256,256]{1,0:T(8,128)(2,1)S(1)}, bf16[256,256]{1,0:T(8,128)(2,1)S(1)}, u32[]{:S(2)}, u32[]{:S(2)}) collective-permute-start(bf16[256,256]{1,0:T(8,128)(2,1)S(1)} %shard_map.42.refs_0_), channel_id=1, source_target_pairs={{0,4},{2,6},{4,0},{6,2},{1,5},{3,7},{5,1},{7,3},{8,12},{10,14},{12... | collective-permute-start | bytes 393224 | tf_op jit(solution)/shard_map/ppermute | solution.py:206
  58.5 13.5 %collective-permute-start.23 = (bf16[256,256]{1,0:T(8,128)(2,1)S(1)}, bf16[256,256]{1,0:T(8,128)(2,1)S(1)}, u32[]{:S(2)}, u32[]{:S(2)}) collective-permute-start(bf16[256,256]{1,0:T(8,128)(2,1)S(1)} %shard_map.42.refs_0_), channel_id=1, source_target_pairs={{0,1},{1,0},{2,3},{3,2},{4,5},{5,4},{6,7},{7,6},{8,9},{9,8},{10,11... | collective-permute-start | bytes 393224 | tf_op jit(solution)/shard_map/ppermute | solution.py:207
  64.7 9.5 %collective-permute-start.20 = (bf16[256,256]{1,0:T(8,128)(2,1)S(1)}, bf16[256,256]{1,0:T(8,128)(2,1)S(1)}, u32[]{:S(2)}, u32[]{:S(2)}) collective-permute-start(bf16[256,256]{1,0:T(8,128)(2,1)S(1)} %collective-permute-done.19.refs_0_), channel_id=1, source_target_pairs={{0,1},{1,0},{2,3},{3,2},{4,5},{5,4},{6,7},{7,6},{8,9},{9,8},{10,11... | collective-permute-start | bytes 393224 | tf_op jit(solution)/shard_map/ppermute | solution.py:207
  67.8 6.5 %collective-permute-start.22 = (bf16[256,256]{1,0:T(8,128)(2,1)S(1)}, bf16[256,256]{1,0:T(8,128)(2,1)S(1)}, u32[]{:S(2)}, u32[]{:S(2)}) collective-permute-start(bf16[256,256]{1,0:T(8,128)(2,1)S(1)} %collective-permute-done.21.refs_1_), channel_id=1, source_target_pairs={{0,1},{1,0},{2,3},{3,2},{4,5},{5,4},{6,7},{7,6},{8,9},{9,8},{10,11... | collective-permute-start | bytes 393224 | tf_op jit(solution)/shard_map/ppermute | solution.py:207
  68.2 8.1 %collective-permute-start.18 = (bf16[256,256]{1,0:T(8,128)(2,1)S(1)}, bf16[256,256]{1,0:T(8,128)(2,1)S(1)}, u32[]{:S(2)}, u32[]{:S(2)}) collective-permute-start(bf16[256,256]{1,0:T(8,128)(2,1)S(1)} %collective-permute-done.17.refs_0_), channel_id=1, source_target_pairs={{0,1},{1,0},{2,3},{3,2},{4,5},{5,4},{6,7},{7,6},{8,9},{9,8},{10,11... | collective-permute-start | bytes 393224 | tf_op jit(solution)/shard_map/ppermute | solution.py:207
